TPU v7x, 512 devices: a whole 4x8x8 slice. The times are simulated.
512 devices in a mesh: dp: 64 (over x, z, core), mp: 8 (over y).
Axes of the slice: x: 4, y: 8, z: 8, core: 2. Of those that a mesh axis runs over, the one named last changes fastest.
Arguments:
- ranges: bfloat16 [8192, 2652], P(('dp', 'mp')), may hold values from 0.0099487305 to 1
- board: int32 [8192, 5], P(('dp', 'mp')), may hold values from 0 to 51, as said below
- targets: bfloat16 [8192, 2652], P(('dp', 'mp')), may hold values from -6 to 6
- w_in: bfloat16 [1536, 2704], P(('mp', 'dp')), may hold values from -0.34570312 to 0.34570312
- w_out: bfloat16 [1536, 2652], P(('mp', 'dp')), may hold values from -0.3046875 to 0.3046875
Outputs:
- predicted: bfloat16 [8192, 2652], P(('dp', 'mp'))
- update_in: float32 [1536, 2704], P(('mp', 'dp'))
- update_out: float32 [1536, 2652], P(('mp', 'dp'))
- loss: float32 [], replicated
Inputs may be any that keep to these rules, and one draw needn't show every extreme that they name: `board`: each row holds 5 different cards.
All inputs are finite; a program needn't handle non-finite values.
Results may differ from a plain program's by a relative error of at most 0.014.
Values may be sent and summed in bfloat16 or wider, within the bound.
A program may use at most 64 MiB of HBM per device.

v0:
```python
import jax
import jax.numpy as jnp
from jax import lax
from jax.sharding import Mesh
from jax.sharding import PartitionSpec as P

CARDS = 52
HIDDEN_SIZE = 1536
DP = ("dp_0", "dp_1", "dp_2")
DP_MP = ("dp_0", "dp_1", "dp_2", "mp")
MP_DP = ("mp", "dp_0", "dp_1", "dp_2")


def laid_out(tiles, dim):
    tiles = jnp.moveaxis(tiles, 0, dim)
    dims = tiles.shape
    return tiles.reshape(*dims[:dim], dims[dim] * dims[dim + 1], *dims[dim + 2 :])


def sent_to_all(array, axis):
    peers = lax.axis_size(axis)
    return lax.all_to_all(
        jnp.broadcast_to(array[None], (peers, *array.shape)), axis, 0, 0, tiled=True
    )


def collect(array, axis, dim):
    return laid_out(sent_to_all(array, axis), dim)


def in_blocks(array, dim, peers):
    before, after = (array.shape[:dim], array.shape[dim + 1 :])
    return jnp.moveaxis(array.reshape(*before, peers, -1, *after), dim, 0)


def sent_and_summed(array, axis, dim):
    peers = lax.axis_size(axis)
    tiles = lax.all_to_all(in_blocks(array, dim, peers), axis, 0, 0, tiled=True)
    return jnp.sum(tiles.astype(jnp.float32), axis=0)


def over_axes(array, axes):
    for axis in axes:
        array = lax.psum(array, axis)
    return array


def huber_terms(error_value):
    magnitude = jnp.abs(error_value)
    return jnp.where(magnitude <= 1.0, 0.5 * error_value * error_value, magnitude - 0.5)


def build_features(all_ranges, all_board, card_count):
    card_ids = jnp.arange(card_count, dtype=jnp.int32)
    onehot_board = jnp.sum(
        (all_board[:, :, None] == card_ids[None, None, :]).astype(jnp.float32), axis=1
    ).astype(jnp.bfloat16)
    return jnp.concatenate([all_ranges, onehot_board], axis=1)


def right_product(left_side, right_block):
    return lax.dot_general(
        left_side, right_block, (((1,), (1,)), ((), ())), preferred_element_type=jnp.float32
    )


def left_product(left_side, right_side):
    return lax.dot_general(
        left_side, right_side, (((0,), (0,)), ((), ())), preferred_element_type=jnp.float32
    )


def body(ranges, board, targets, w_in, w_out):
    mp_count = lax.axis_size("mp")
    dp_count = lax.axis_size(DP)
    stored_rows = ranges.shape[0]
    value_width = w_out.shape[1]
    all_ranges, all_board = (collect(ranges, "mp", 0), collect(board, "mp", 0))
    features = build_features(all_ranges, all_board, CARDS)
    local_in = lax.all_gather(w_in, DP, axis=0, tiled=True)
    preact = right_product(features, local_in)
    hidden = jax.nn.gelu(preact).astype(jnp.bfloat16)
    local_out = lax.all_gather(w_out, DP, axis=0, tiled=True)
    partial_value = jnp.dot(hidden, local_out, preferred_element_type=jnp.float32)
    stacked = partial_value.astype(jnp.bfloat16).reshape(mp_count, stored_rows, value_width)
    received = lax.all_to_all(stacked, "mp", split_axis=0, concat_axis=0, tiled=True)
    summed = jnp.sum(received.astype(jnp.float32), axis=0)
    error_value = summed - targets.astype(jnp.float32)
    own_grad = jnp.clip(error_value, -1.0, 1.0).astype(jnp.bfloat16)
    out_grad = collect(own_grad, "mp", 0)
    predicted = summed.astype(jnp.bfloat16)
    loss_part = jnp.sum(huber_terms(error_value))
    grad_out = sent_and_summed(left_product(hidden, out_grad).astype(jnp.bfloat16), DP, 0)
    hidden_grad = right_product(out_grad, local_out)
    unused_value, gelu_back = jax.vjp(jax.nn.gelu, preact)
    preact_grad = gelu_back(hidden_grad)[0].astype(jnp.bfloat16)
    grad_in = sent_and_summed(left_product(preact_grad, features).astype(jnp.bfloat16), DP, 0)
    square_part = jnp.sum(grad_in * grad_in) + jnp.sum(grad_out * grad_out)
    loss_total, square_total = (over_axes(loss_part, DP_MP), over_axes(square_part, DP_MP))
    count_params = HIDDEN_SIZE * (w_in.shape[1] + value_width)
    scale = lax.rsqrt(square_total / count_params + 1e-06)
    loss = loss_total / (stored_rows * mp_count * dp_count * value_width)
    return (predicted, grad_in * scale, grad_out * scale, loss)


def solution(mesh):
    split = Mesh(mesh.devices.reshape(4, 8, 2, mesh.shape["mp"]), ("dp_0", "dp_1", "dp_2", "mp"))
    placed = (P(DP_MP, None), P(DP_MP, None), P(DP_MP, None), P(MP_DP, None), P(MP_DP, None))
    return jax.shard_map(
        body,
        mesh=split,
        in_specs=placed,
        out_specs=(P(DP_MP, None), P(MP_DP, None), P(MP_DP, None), P()),
        check_vma=False,
    )
```

profile of v0, /device:TPU:1, one launch (start us, length us, event | category | flops | bytes accessed | tf_op | source)
XLA Modules:
  0.0 321.7 jit_solution(1523296444616732126)
XLA Ops:
  0.6 0.0 copy-start.2
  0.6 0.7 broadcast_in_dim.7
  1.3 14.3 %all_to_all.30 = s32[8,16,5]{1,2,0:T(8,128)S(1)} all-to-all(s32[8,16,5]{1,2,0:T(8,128)S(1)} %broadcast_in_dim.7), channel_id=1, replica_groups=mesh['dp_0'=4,'dp_1'=8,'dp_2'=2,'mp'=8] {'mp'}, dimensions={0} | all-to-all | bytes 5120 | tf_op jit(solution)/shard_map/all_to_all | solution.py:22
  15.6 1.8 broadcast_in_dim.6
  17.5 3.5 %all-to-all-start = ((bf16[8,16,2652]{2,1,0:T(8,128)(2,1)}), bf16[8,16,2652]{2,1,0:T(8,128)(2,1)S(1)}, u32[]{:S(2)}, u32[]{:S(2)}) async-start(bf16[8,16,2652]{2,1,0:T(8,128)(2,1)} %broadcast_in_dim.6), calls=%async_computation | async-start | bytes 1376256 | tf_op jit(solution)/shard_map/all_to_all | solution.py:22
  21.0 0.0 copy-done.2
  21.0 58.7 %all-gather = bf16[64,3,2704]{2,1,0:T(4,128)(2,1)S(1)} all-gather(bf16[1,3,2704]{2,1,0:T(4,128)(2,1)S(1)} %bitcast.17), channel_id=1, replica_groups=mesh['dp_0'=4,'dp_1'=8,'dp_2'=2,'mp'=8] {'dp_0','dp_1','dp_2'}, dimensions={0}, use_global_device_ids=true | all-gather | bytes 1054560 | tf_op jit(solution)/shard_map/all_gather | solution.py:80
  79.7 0.0 copy-start.3
  79.7 1.7 reshape.33
  81.4 0.0 copy-done.3
  81.4 49.8 %all-gather.1 = bf16[64,3,2652]{2,1,0:T(4,128)(2,1)S(1)} all-gather(bf16[1,3,2652]{2,1,0:T(4,128)(2,1)S(1)} %bitcast.18), channel_id=1, replica_groups=mesh['dp_0'=4,'dp_1'=8,'dp_2'=2,'mp'=8] {'dp_0','dp_1','dp_2'}, dimensions={0}, use_global_device_ids=true | all-gather | bytes 1034280 | tf_op jit(solution)/shard_map/all_gather | solution.py:83
  131.2 0.9 reshape.35
  132.1 0.1 eq.15
  132.2 0.1 copy.17
  132.4 0.0 all-to-all-done
  132.4 0.0 copy-start
  132.4 1.9 fusion
  134.3 0.7 convolution_convert_fusion.2
  135.0 0.3 copy.18
  135.3 0.0 copy-start.1
  135.3 28.0 %all_to_all.31 = bf16[8,16,2652]{2,1,0:T(8,128)(2,1)S(1)} all-to-all(bf16[8,16,2652]{2,1,0:T(8,128)(2,1)S(1)} %bitcast.16), channel_id=1, replica_groups=mesh['dp_0'=4,'dp_1'=8,'dp_2'=2,'mp'=8] {'mp'}, dimensions={0} | all-to-all | bytes 1357824 | tf_op jit(solution)/shard_map/all_to_all | solution.py:86
  163.4 0.1 convert_reduce_fusion.2
  163.5 0.0 copy-done.1
  163.5 1.3 fusion.2
  164.8 0.0 copy-done
  164.8 22.8 %all_to_all.32 = bf16[8,16,2652]{2,1,0:T(8,128)(2,1)S(1)} all-to-all(bf16[8,16,2652]{2,1,0:T(8,128)(2,1)S(1)} %broadcast_in_dim.8), channel_id=1, replica_groups=mesh['dp_0'=4,'dp_1'=8,'dp_2'=2,'mp'=8] {'mp'}, dimensions={0} | all-to-all | bytes 1357824 | tf_op jit(solution)/shard_map/all_to_all | solution.py:22
  187.6 0.4 convolution_convert_fusion
  188.0 1.3 reshape.31
  189.4 6.4 %all-to-all-start.5 = ((bf16[64,3,2652]{2,1,0:T(4,128)(2,1)}), bf16[64,3,2652]{2,1,0:T(4,128)(2,1)S(1)}, u32[]{:S(2)}, u32[]{:S(2)}) async-start(bf16[64,3,2652]{2,1,0:T(4,128)(2,1)} %reshape.31), calls=%async_computation.5 | async-start | bytes 2752512 | tf_op jit(solution)/shard_map/all_to_all | solution.py:38
  195.8 3.4 %convolution_convert_fusion.1 = bf16[192,2704]{1,0:T(8,128)(2,1)} fusion(bf16[128,52]{1,0:T(8,128)(2,1)S(1)} %copy.17, bf16[128,2652]{1,0:T(8,128)(2,1)} %bitcast.15, f32[128,192]{0,1:T(8,128)S(1)} %fusion, bf16[128,2652]{1,0:T(8,128)(2,1)S(1)} %bitcast.13, bf16[192,2652]{1,0:T(8,128)(2,1)S(1)} %reshape.35), kind=kOutput, calls=%fused_computation.1 | convolution fusion | flops 265653248 | bytes 3526144 | tf_op jit(solution)/shard_map/dot_general | solution.py:68
  199.2 3.6 %reshape.30 = bf16[64,3,2704]{2,1,0:T(4,128)(2,1)} reshape(bf16[192,2704]{1,0:T(8,128)(2,1)} %convolution_convert_fusion.1) | data formatting | bytes 2076672 | tf_op jit(solution)/shard_map/reshape | solution.py:33
  202.8 28.6 %all-to-all-done.5 = bf16[64,3,2652]{2,1,0:T(4,128)(2,1)S(1)} async-done(((bf16[64,3,2652]{2,1,0:T(4,128)(2,1)}), bf16[64,3,2652]{2,1,0:T(4,128)(2,1)S(1)}, u32[]{:S(2)}, u32[]{:S(2)}) %all-to-all-start.5) | async-done | bytes 1018400 | tf_op jit(solution)/shard_map/all_to_all | solution.py:38
  231.3 6.2 %all-to-all-start.4 = ((bf16[64,3,2704]{2,1,0:T(4,128)(2,1)}), bf16[64,3,2704]{2,1,0:T(4,128)(2,1)S(1)}, u32[]{:S(2)}, u32[]{:S(2)}) async-start(bf16[64,3,2704]{2,1,0:T(4,128)(2,1)} %reshape.30), calls=%async_computation.4 | async-start | bytes 2883584 | tf_op jit(solution)/shard_map/all_to_all | solution.py:38
  237.5 0.6 convert_reduce_fusion.1
  238.0 0.6 multiply_reduce_fusion.1
  238.7 35.8 %all-to-all-done.4 = bf16[64,3,2704]{2,1,0:T(4,128)(2,1)S(1)} async-done(((bf16[64,3,2704]{2,1,0:T(4,128)(2,1)}), bf16[64,3,2704]{2,1,0:T(4,128)(2,1)S(1)}, u32[]{:S(2)}, u32[]{:S(2)}) %all-to-all-start.4) | async-done | bytes 1038368 | tf_op jit(solution)/shard_map/all_to_all | solution.py:38
  274.4 0.6 convert_reduce_fusion
  275.0 0.6 multiply_reduce_fusion
  276.9 9.5 %all-reduce.2 = (f32[]{:T(128)}, f32[]{:T(128)}) all-reduce(f32[]{:T(128)S(6)} %add.34, f32[]{:T(128)} %get-tuple-element.12), channel_id=1, replica_groups=mesh['dp_0'=4,'dp_1'=8,'dp_2'=2,'mp'=8] {'dp_0'}, use_global_device_ids=true, to_apply=%region_6.7 | all-reduce | flops 2 | bytes 16 | tf_op jit(solution)/shard_map/psum | solution.py:44
  286.4 11.4 %all-reduce.1 = (f32[]{:T(128)}, f32[]{:T(128)}) all-reduce(f32[]{:T(128)} %get-tuple-element.8, f32[]{:T(128)} %get-tuple-element.9), channel_id=1, replica_groups=mesh['dp_0'=4,'dp_1'=8,'dp_2'=2,'mp'=8] {'dp_1'}, use_global_device_ids=true, to_apply=%region_7.8 | all-reduce | flops 2 | bytes 16 | tf_op jit(solution)/shard_map/psum | solution.py:44
  297.8 8.6 %all-reduce.3 = (f32[]{:T(128)}, f32[]{:T(128)}) all-reduce(f32[]{:T(128)} %get-tuple-element.6, f32[]{:T(128)} %get-tuple-element.7), channel_id=1, replica_groups=mesh['dp_0'=4,'dp_1'=8,'dp_2'=2,'mp'=8] {'dp_2'}, use_global_device_ids=true, to_apply=%region_8.9 | all-reduce | flops 2 | bytes 16 | tf_op jit(solution)/shard_map/psum | solution.py:44
  306.4 11.6 %all-reduce = (f32[]{:T(128)}, f32[]{:T(128)}) all-reduce(f32[]{:T(128)} %get-tuple-element.10, f32[]{:T(128)} %get-tuple-element.11), channel_id=1, replica_groups=mesh['dp_0'=4,'dp_1'=8,'dp_2'=2,'mp'=8] {'mp'}, use_global_device_ids=true, to_apply=%region_9.10 | all-reduce | flops 2 | bytes 16 | tf_op jit(solution)/shard_map/psum | solution.py:44
  318.7 0.6 broadcast_multiply_fusion.1
  319.3 0.6 broadcast_multiply_fusion
  (3 shorter events, 0.1 us)
Async XLA Ops:
  0.6 20.4 %copy-start.2 = (bf16[3,2704]{1,0:T(4,128)(2,1)S(1)}, bf16[3,2704]{1,0:T(4,128)(2,1)}, u32[]{:S(2)}) copy-start(bf16[3,2704]{1,0:T(4,128)(2,1)} %param.8) | copy-start | bytes 48676
  17.5 114.9 %all-to-all-start = ((bf16[8,16,2652]{2,1,0:T(8,128)(2,1)}), bf16[8,16,2652]{2,1,0:T(8,128)(2,1)S(1)}, u32[]{:S(2)}, u32[]{:S(2)}) async-start(bf16[8,16,2652]{2,1,0:T(8,128)(2,1)} %broadcast_in_dim.6), calls=%async_computation | async-start | bytes 1376256 | tf_op jit(solution)/shard_map/all_to_all | solution.py:22
  79.7 1.7 copy-start.3
  132.4 32.5 %copy-start = (bf16[8,16,2652]{2,1,0:T(8,128)(2,1)}, bf16[8,16,2652]{2,1,0:T(8,128)(2,1)S(1)}, u32[]{:S(2)}) copy-start(bf16[8,16,2652]{2,1,0:T(8,128)(2,1)S(1)} %all-to-all-done) | copy-start | bytes 2036740
  135.3 28.1 %copy-start.1 = (bf16[16,2652]{1,0:T(8,128)(2,1)S(1)}, bf16[16,2652]{1,0:T(8,128)(2,1)}, u32[]{:S(2)}) copy-start(bf16[16,2652]{1,0:T(8,128)(2,1)} %param.7) | copy-start | bytes 254596
  189.4 41.9 %all-to-all-start.5 = ((bf16[64,3,2652]{2,1,0:T(4,128)(2,1)}), bf16[64,3,2652]{2,1,0:T(4,128)(2,1)S(1)}, u32[]{:S(2)}, u32[]{:S(2)}) async-start(bf16[64,3,2652]{2,1,0:T(4,128)(2,1)} %reshape.31), calls=%async_computation.5 | async-start | bytes 2752512 | tf_op jit(solution)/shard_map/all_to_all | solution.py:38
  231.3 43.1 %all-to-all-start.4 = ((bf16[64,3,2704]{2,1,0:T(4,128)(2,1)}), bf16[64,3,2704]{2,1,0:T(4,128)(2,1)S(1)}, u32[]{:S(2)}, u32[]{:S(2)}) async-start(bf16[64,3,2704]{2,1,0:T(4,128)(2,1)} %reshape.30), calls=%async_computation.4 | async-start | bytes 2883584 | tf_op jit(solution)/shard_map/all_to_all | solution.py:38
where the time goes:
time: 325 us; the launch traced here: 322 us
  blocking collectives  215 us (66%)
  waiting for transfers between devices  64.3 us (20%)
  starting transfers between devices  16.1 us (5%)
  local copies, waits for them, and re-layouts  10.7 us (3%)
  matrix products  6.4 us (2%)
  other arithmetic  5.09 us (2%)
  between operations  4.53 us (1%)
    all_to_all x2, waiting for transfers between devices, sent_and_summed(): tiles = lax.all_to_all(in_blocks(array, dim, peers), axis, 0, 0, tiled=True)  64.3 us
    all_gather x1, blocking collectives, body(): local_in = lax.all_gather(w_in, DP, axis=0, tiled=True)  58.7 us
    all_gather x1, blocking collectives, body(): local_out = lax.all_gather(w_out, DP, axis=0, tiled=True)  49.8 us
    psum x4, blocking collectives, over_axes(): array = lax.psum(array, axis)  41 us
    all_to_all x2, blocking collectives, sent_to_all(): lax.all_to_all(jnp.broadcast_to(array[None], (peers, *array.shape)), axis...  37.1 us
    all_to_all x1, blocking collectives, body(): lax.all_to_all(stacked, 'mp', split_axis=0, concat_axis=0, tiled=True)  28 us
    all_to_all x2, starting transfers between devices, sent_and_summed(): tiles = lax.all_to_all(in_blocks(array, dim, peers), axis, 0, 0, tiled=True)  12.6 us
  transfers between devices with their start and end apart: 3, of which 2 were waited for; matrix products, arithmetic and copies ran while one was open for 3% of the time, Pallas kernels for 0%

commit v1 on v0

v1 whole, which is shorter than its diff:
```python
import functools

import jax
import jax.numpy as jnp
from jax import lax
from jax.experimental import pallas as pl
from jax.experimental.pallas import tpu as pltpu
from jax.sharding import PartitionSpec as P

MESH = pl.DeviceIdType.MESH
BF16, F32 = jnp.bfloat16, jnp.float32
NX, NZ, NY, NC = 4, 8, 8, 2
ROWS, GROUP, STATES = 3, 24, 16
HALF = 1408
INW, OUTW, HIDDEN, BATCH = 2704, 2652, 1536, 8192
LONG, SHORT = 4, 3
GELU_A, GELU_B = 0.7978845608028654, 0.044715


def nt(a, b):
    return lax.dot_general(a, b, (((1,), (1,)), ((), ())), preferred_element_type=F32)


def nn(a, b):
    return lax.dot_general(a, b, (((1,), (0,)), ((), ())), preferred_element_type=F32)


def kernel(
    ranges, board, targets, w_in, w_out,
    predicted, update_in, update_out, loss,
    stage, rows8, pack, weights, feats, grads_out,
    partial, rs_send, rs_long, rs_short, target_pad,
    hold, mine, cross, crossed, z_send, z_long, z_short, x_send, x_recv,
    ar_send, ar_recv,
    s_wx, r_wx, s_f, r_f, s_wz, r_wz, s_wd, r_wd, s_rs, r_rs, s_ag, r_ag,
    s_gd, r_gd, s_gz, r_gz, s_gx, r_gx, s_ar, r_ar,
):
    d = lax.axis_index("dp")
    y = lax.axis_index("mp")
    c = lax.rem(d, 2)
    z = lax.rem(lax.div(d, 2), NZ)
    x = lax.div(d, 2 * NZ)
    sign = 1 - 2 * c
    me8 = x * 2 + c

    def around(base, step, n):
        return lax.rem(base + step + n, n)

    def at_dev(x_, z_, c_, y_):
        return {"dp": (x_ * NZ + z_) * 2 + c_, "mp": y_}

    def peer(k):
        return around(x, k // 2, NX), (c if k % 2 == 0 else 1 - c)

    started = []

    def send(src, dst, s, r, device):
        copy = pltpu.make_async_remote_copy(
            src_ref=src, dst_ref=dst, send_sem=s, recv_sem=r, device_id=device, device_id_type=MESH
        )
        copy.start()
        started.append(copy)
        return copy

    y_long, y_short = around(y, sign, NY), around(y, -sign, NY)
    z_up, z_down = around(z, sign, NZ), around(z, -sign, NZ)
    to_y = (at_dev(x, z, c, y_long), at_dev(x, z, c, y_short))
    to_z = (at_dev(x, z_up, c, y), at_dev(x, z_down, c, y))
    partner = at_dev(x, z, 1 - c, y)

    barrier = pltpu.get_barrier_semaphore()
    near = [to_y[0], to_y[1], to_z[0], to_z[1]]
    for k in range(1, 8):
        px, pc = peer(k)
        near.append(at_dev(px, z, pc, y))
    for device in near:
        pl.semaphore_signal(barrier, inc=1, device_id=device, device_id_type=MESH)

    for i, (w, width) in enumerate(((w_in, INW), (w_out, OUTW))):
        stage[i, 0] = w[:, :HALF]
        stage[i, 1] = jnp.zeros((ROWS, HALF), BF16)
        stage[i, 1, :, : width - HALF] = w[:, HALF:]
    feats[0, y] = ranges[:, :HALF]
    cards = lax.broadcasted_iota(jnp.int32, (STATES, HALF), 1) - (OUTW - HALF)
    shown = jnp.zeros((STATES, HALF), F32)
    for k in range(5):
        shown = shown + (board[:, k : k + 1] == cards).astype(F32)
    tail = jnp.concatenate([ranges[:, HALF:].astype(F32), jnp.zeros((STATES, 2 * HALF - OUTW), F32)], axis=1)
    feats[1, y] = (tail + shown).astype(BF16)
    target_pad[...] = jnp.zeros(target_pad.shape, F32)
    target_pad[0] = targets[:, :HALF].astype(F32)
    target_pad[1, :, : OUTW - HALF] = targets[:, HALF:].astype(F32)

    pl.semaphore_wait(barrier, len(near))

    wx = [[None] * 8, [None] * 8]
    for i in range(2):
        for k in range(1, 8):
            px, pc = peer(k)
            wx[i][k] = send(stage.at[i, pc], rows8.at[i, me8], s_wx.at[i, k], r_wx.at[i, k], at_dev(px, z, pc, y))
        rows8[i, me8] = stage[i, c]

    def ring_gather(block_of, pos, n, to, s, r, arrived=lambda origin, j: None):
        copies = {}

        def step(k):
            for way, steps in ((0, LONG), (1, SHORT)):
                if k >= 1 and k - 1 < steps:
                    copies[way, k - 1].wait_recv()
                move = -k * sign if way == 0 else k * sign
                origin = around(pos, move, n)
                if k < steps:
                    block = block_of(origin)
                    copies[way, k] = send(block, block, s(way * LONG + k), r(way * LONG + k), to[way])
                if k >= 1 and k - 1 < steps:
                    arrived(origin, way * LONG + k)

        return step

    f_steps = [
        ring_gather(
            lambda o, h=h: feats.at[h, o], y, NY, to_y, lambda j, h=h: s_f.at[h, j], lambda j, h=h: r_f.at[h, j]
        )
        for h in range(2)
    ]
    for h in range(2):
        f_steps[h](0)

    across = []

    def to_partner(i, origin, j):
        block = weights.at[i, c, origin]
        across.append(send(block, block, s_wd.at[i, j], r_wd.at[i, j], partner))

    w_steps = []
    for i in range(2):
        for k in range(1, 8):
            wx[i][k].wait_recv()
        for j in range(8):
            pack[i, ROWS * j : ROWS * (j + 1)] = rows8[i, j].astype(F32)
        weights[i, c, z] = pack[i].astype(BF16)
        w_steps.append(
            ring_gather(
                lambda o, i=i: weights.at[i, c, o], z, NZ, to_z,
                lambda j, i=i: s_wz.at[i, j], lambda j, i=i: r_wz.at[i, j],
                lambda o, j, i=i: to_partner(i, o, j),
            )
        )
        w_steps[i](0)
        to_partner(i, z, 0)
    for k in range(1, LONG + 1):
        w_steps[0](k)
        f_steps[0](k)
        f_steps[1](k)
        w_steps[1](k)
    for copy in across:
        copy.wait_recv()

    def w_half(i, h):
        return weights[i, h].reshape(NZ * GROUP, HALF)

    def f_half(h):
        return feats[h].reshape(NY * STATES, HALF)

    pre = nt(w_half(0, 0), f_half(0)) + nt(w_half(0, 1), f_half(1))
    tanh = jnp.tanh(GELU_A * (pre + GELU_B * pre * pre * pre))
    hidden = 0.5 * pre * (1.0 + tanh)
    slope = 0.5 * (1.0 + tanh) + 0.5 * pre * (1.0 - tanh * tanh) * (GELU_A * (1.0 + 3.0 * GELU_B * pre * pre))
    hold[0] = hidden
    hold[1] = slope
    hidden_t = hidden.T.astype(BF16)
    for h in range(2):
        partial[h] = nn(hidden_t, w_half(1, h)).reshape(NY, STATES, HALF)

    def ring_sum(term, pos, n, to, out, came, s, r):
        copies = {}

        def step(k):
            for way, steps in ((0, LONG), (1, SHORT)):
                if k < steps:
                    move = (steps - k) * sign if way == 0 else -(steps - k) * sign
                    value = term(around(pos, move, n))
                    if k >= 1:
                        copies[way, k - 1].wait_recv()
                        value = value + came(way, k - 1)[...].astype(F32)
                    j = way * LONG + k
                    out(j)[...] = value.astype(BF16)
                    copies[way, k] = send(out(j), came(way, k), s(j), r(j), to[way])

        def last():
            value = term(pos)
            for way, steps in ((0, LONG), (1, SHORT)):
                copies[way, steps - 1].wait_recv()
                value = value + came(way, steps - 1)[...].astype(F32)
            return value

        return step, last

    rs = [
        ring_sum(
            lambda t, h=h: partial[h, t], y, NY, to_y, lambda j, h=h: rs_send.at[h, j],
            lambda way, k, h=h: (rs_long, rs_short)[way].at[h, k],
            lambda j, h=h: s_rs.at[h, j], lambda j, h=h: r_rs.at[h, j],
        )
        for h in range(2)
    ]
    for k in range(LONG):
        for h in range(2):
            rs[h][0](k)
    g_steps = []
    lost = jnp.zeros((1, 1), F32)
    for h in range(2):
        summed = rs[h][1]()
        error = summed - target_pad[h]
        size = jnp.abs(error)
        terms = jnp.where(size <= 1.0, 0.5 * error * error, size - 0.5)
        lost = lost + jnp.sum(terms, keepdims=True)
        grads_out[h, y] = jnp.clip(error, -1.0, 1.0).astype(BF16)
        if h == 0:
            predicted[:, :HALF] = summed.astype(BF16)
        else:
            predicted[:, HALF:] = summed[:, : OUTW - HALF].astype(BF16)
        g_steps.append(
            ring_gather(
                lambda o, h=h: grads_out.at[h, o], y, NY, to_y,
                lambda j, h=h: s_ag.at[h, j], lambda j, h=h: r_ag.at[h, j],
            )
        )
        g_steps[h](0)
    for k in range(1, LONG + 1):
        for h in range(2):
            g_steps[h](k)

    def g_half(h):
        return grads_out[h].reshape(NY * STATES, HALF)

    def weight_grad(g, left, right):
        cross[g] = nn(left, right(1 - c)).astype(BF16).reshape(NZ, GROUP, HALF)
        copy = send(cross.at[g], crossed.at[g], s_gd.at[g], r_gd.at[g], partner)
        mine[g] = nn(left, right(c)).reshape(NZ, GROUP, HALF)
        return copy

    def z_ring(g):
        return ring_sum(
            lambda t: mine[g, t] + crossed[g, t].astype(F32), z, NZ, to_z, lambda j: z_send.at[g, j],
            lambda way, k: (z_long, z_short)[way].at[g, k],
            lambda j: s_gz.at[g, j], lambda j: r_gz.at[g, j],
        )

    over = [weight_grad(1, hold[0].astype(BF16), g_half)]
    hidden_grad = nt(w_half(1, 0), g_half(0)) + nt(w_half(1, 1), g_half(1))
    pre_grad = (hidden_grad * hold[1]).astype(BF16)
    over[0].wait_recv()
    zr = {1: z_ring(1)}
    zr[1][0](0)
    over.append(weight_grad(0, pre_grad, f_half))
    over[1].wait_recv()
    zr[0] = z_ring(0)
    zr[0][0](0)
    for k in range(1, LONG):
        zr[1][0](k)
        zr[0][0](k)
    gx = {}
    for g in (1, 0):
        total = zr[g][1]()
        for j in range(8):
            x_send[g, j] = total[ROWS * j : ROWS * (j + 1)].astype(BF16)
        for k in range(1, 8):
            px, pc = peer(k)
            gx[g, k] = send(
                x_send.at[g, px * 2 + pc], x_recv.at[g, me8], s_gx.at[g, k], r_gx.at[g, k], at_dev(px, z, pc, y)
            )
        x_recv[g, me8] = x_send[g, me8]
    squares = jnp.zeros((1, 1), F32)
    for g in (1, 0):
        for k in range(1, 8):
            gx[g, k].wait_recv()
        for h in range(2):
            own = x_recv[g, h].astype(F32)
            for px in range(1, NX):
                own = own + x_recv[g, 2 * px + h].astype(F32)
            hold_g = (update_in, update_out)[g]
            width = (INW, OUTW)[g]
            if h == 0:
                hold_g[:, :HALF] = own
            else:
                own = own[:, : width - HALF]
                hold_g[:, HALF:] = own
            squares = squares + jnp.sum(own * own, keepdims=True)

    lane = lax.broadcasted_iota(jnp.int32, (1, 128), 1)
    total = jnp.where(lane == 0, squares, jnp.where(lane == 1, lost, 0.0))
    for phase in range(3):
        ar_send[phase] = total
        slot = (me8, z, y)[phase]
        ar_recv[phase, slot] = total
        copies = []
        for k in range(1, 8):
            if phase == 0:
                px, pc = peer(k)
                device = at_dev(px, z, pc, y)
            elif phase == 1:
                device = at_dev(x, around(z, k, NZ), c, y)
            else:
                device = at_dev(x, z, c, around(y, k, NY))
            copies.append(send(ar_send.at[phase], ar_recv.at[phase, slot], s_ar.at[phase, k], r_ar.at[phase, k], device))
        for copy in copies:
            copy.wait_recv()
        total = jnp.sum(ar_recv[phase], axis=0)
    loss[...] = total[:, 1:2] / (BATCH * OUTW)
    scale = lax.rsqrt(total[:, 0:1] / (HIDDEN * (INW + OUTW)) + 1e-6)
    update_in[...] = update_in[...] * scale
    update_out[...] = update_out[...] * scale
    for copy in started:
        copy.wait_send()


def body(ranges, board, targets, w_in, w_out):
    vmem = pl.BlockSpec(memory_space=pltpu.VMEM)
    dma = pltpu.SemaphoreType.DMA
    scratch = [
        pltpu.VMEM((2, 2, ROWS, HALF), BF16),
        pltpu.VMEM((2, 8, ROWS, HALF), BF16),
        pltpu.VMEM((2, GROUP, HALF), F32),
        pltpu.VMEM((2, 2, NZ, GROUP, HALF), BF16),
        pltpu.VMEM((2, NY, STATES, HALF), BF16),
        pltpu.VMEM((2, NY, STATES, HALF), BF16),
        pltpu.VMEM((2, NY, STATES, HALF), F32),
        pltpu.VMEM((2, 7, STATES, HALF), BF16),
        pltpu.VMEM((2, LONG, STATES, HALF), BF16),
        pltpu.VMEM((2, SHORT, STATES, HALF), BF16),
        pltpu.VMEM((2, STATES, HALF), F32),
        pltpu.VMEM((2, NZ * GROUP, NY * STATES), F32),
        pltpu.VMEM((2, NZ, GROUP, HALF), F32),
        pltpu.VMEM((2, NZ, GROUP, HALF), BF16),
        pltpu.VMEM((2, NZ, GROUP, HALF), BF16),
        pltpu.VMEM((2, 7, GROUP, HALF), BF16),
        pltpu.VMEM((2, LONG, GROUP, HALF), BF16),
        pltpu.VMEM((2, SHORT, GROUP, HALF), BF16),
        pltpu.VMEM((2, 8, ROWS, HALF), BF16),
        pltpu.VMEM((2, 8, ROWS, HALF), BF16),
        pltpu.VMEM((3, 1, 128), F32),
        pltpu.VMEM((3, 8, 1, 128), F32),
    ]
    for shape in ((2, 8), (2, 7), (2, 7), (2, 8), (2, 7), (2, 7), (2,), (2, 7), (2, 8), (3, 8)):
        scratch += [dma(shape), dma(shape)]
    out = pl.pallas_call(
        kernel,
        name="step",
        out_shape=(
            jax.ShapeDtypeStruct((STATES, OUTW), BF16),
            jax.ShapeDtypeStruct((ROWS, INW), F32),
            jax.ShapeDtypeStruct((ROWS, OUTW), F32),
            jax.ShapeDtypeStruct((1, 1), F32),
        ),
        in_specs=[vmem] * 5,
        out_specs=(vmem,) * 4,
        scratch_shapes=scratch,
        compiler_params=pltpu.CompilerParams(
            collective_id=0, has_side_effects=True, vmem_limit_bytes=48 * 1024 * 1024
        ),
    )(ranges, board, targets, w_in, w_out)
    return out[0], out[1], out[2], out[3][0, 0]


def solution(mesh):
    rows, units = P(("dp", "mp"), None), P(("mp", "dp"), None)
    return jax.shard_map(
        body,
        mesh=mesh,
        in_specs=(rows, rows, rows, units, units),
        out_specs=(rows, units, units, P()),
        check_vma=False,
    )
```

time: 325 us -> 109 us (0.34)
  blocking collectives: 215 us -> 0 us
  Pallas kernels: 0 us -> 100 us
  waiting for transfers between devices: 64.3 us -> 0 us
  starting transfers between devices: 16.1 us -> 0 us
  matrix products: 6.4 us -> 0 us
  other arithmetic: 5.09 us -> 0 us
  local copies, waits for them, and re-layouts: 10.7 us -> 5.88 us
    all_gather x2 -> x0, blocking collectives: 108 us -> none  [the longest x1 58.7 us: body(): local_in = lax.all_gather(w_in, DP, axis=0, tiled=True)]
    pallas_call x0 -> x1, Pallas kernels: none -> 100 us  [body(): pl.pallas_call(kernel, name='step', out_shape=(jax.ShapeDtypeStruct((STAT...]
    all_to_all x3 -> x0, blocking collectives: 65.1 us -> none  [the longest x2 37.1 us: sent_to_all(): lax.all_to_all(jnp.broadcast_to(array[None], (peers, *array.shape)), axis...]
    all_to_all x3 -> x0, waiting for transfers between devices: 64.3 us -> none  [the longest x2 64.3 us: sent_and_summed(): tiles = lax.all_to_all(in_blocks(array, dim, peers), axis, 0, 0, tiled=True)]
    psum x4 -> x0, blocking collectives: 41 us -> none  [over_axes(): array = lax.psum(array, axis)]
    all_to_all x3 -> x0, starting transfers between devices: 16.1 us -> none  [the longest x2 12.6 us: sent_and_summed(): tiles = lax.all_to_all(in_blocks(array, dim, peers), axis, 0, 0, tiled=True)]
    dot_general x4 -> x0, matrix products: 6.4 us -> none  [the longest x2 3.8 us: left_product(): lax.dot_general(left_side, right_side, (((0,), (0,)), ((), ())), preferre...]
    reshape x2 -> x0, local copies, waits for them, and re-layouts: 4.95 us -> none  [in_blocks(): return jnp.moveaxis(array.reshape(*before, peers, -1, *after), dim, 0)]
  transfers between devices with their start and end apart: 3 -> 0, of which waited for: 2 -> 0; matrix products, arithmetic and copies ran while one was open for 3% -> 0% of each run, Pallas kernels for 0% -> 0%
where the time goes in v1:
time: 109 us; the launch traced here: 108 us
  Pallas kernels  100 us (92%)
  local copies, waits for them, and re-layouts  5.88 us (5%)
  between operations  2.39 us (2%)
    pallas_call x1, Pallas kernels, body(): pl.pallas_call(kernel, name='step', out_shape=(jax.ShapeDtypeStruct((STAT...  100 us
    unnamed x12, local copies, waits for them, and re-layouts  5.88 us

profile of v1, /device:TPU:1, one launch (start us, length us, event | category | flops | bytes accessed | tf_op | source)
XLA Modules:
  0.0 108.3 jit_solution(3362152803504159263)
XLA Ops:
  0.6 0.8 copy.9.board
  1.4 0.0 copy-start
  1.4 0.9 copy-done
  2.3 0.0 copy-start.1
  2.3 0.9 copy-done.1
  3.2 0.0 copy-start.2
  3.2 0.7 copy-done.2
  3.9 0.0 copy-start.3
  3.9 0.7 copy-done.3
  4.6 100.0 %step.1 = (bf16[16,2652]{1,0:T(8,128)(2,1)S(1)}, f32[3,2704]{1,0:T(4,128)S(1)}, f32[3,2652]{1,0:T(4,128)S(1)}, f32[1,1]{1,0:T(1,128)}) custom-call(bf16[16,2652]{1,0:T(8,128)(2,1)S(1)} %copy-done, s32[16,5]{1,0:T(8,128)S(1)} %copy.9.board, bf16[16,2652]{1,0:T(8,128)(2,1)S(1)} %copy-done.1, bf16[3,2704]{1,0:T(4,128)(2,1)S(1)} %copy-done.2, ...), custom_call_target="tpu_custom_call" | custom-call | tf_op jit(solution)/shard_map/step/pallas_call | solution.py:347
  104.7 0.6 copy.14
  105.3 0.6 copy.15
  105.9 0.6 copy.16
Async XLA Ops:
  1.4 0.9 copy-start
  2.3 0.9 copy-start.1
  3.2 0.7 copy-start.2
  3.9 0.7 copy-start.3

commit v2 on v1

v2 whole, which is shorter than its diff:
```python
import functools

import jax
import jax.numpy as jnp
from jax import lax
from jax.experimental import pallas as pl
from jax.experimental.pallas import tpu as pltpu
from jax.sharding import PartitionSpec as P

PROFILE = False
VMEM_STEP = 67043328
MESH = pl.DeviceIdType.MESH
BF16, F32 = jnp.bfloat16, jnp.float32
NX, NZ, NY, NC = 4, 8, 8, 2
ROWS, GROUP, STATES = 3, 24, 16
HALF = 1408
INW, OUTW, HIDDEN, BATCH = 2704, 2652, 1536, 8192
LONG, SHORT = 4, 3
GELU_A, GELU_B = 0.7978845608028654, 0.044715


def nt(a, b):
    return lax.dot_general(a, b, (((1,), (1,)), ((), ())), preferred_element_type=F32)


def nn(a, b):
    return lax.dot_general(a, b, (((1,), (0,)), ((), ())), preferred_element_type=F32)


O_WIDTH = 2688
F_CHUNKS = tuple((h, slice(128 * a, 128 * b)) for h in range(2) for a, b in ((0, 6), (6, 11)))
O_CHUNKS = tuple(
    (h, slice(128 * a, 128 * b)) for h, cuts in enumerate((((0, 6), (6, 11)), ((0, 5), (5, 10)))) for a, b in cuts
)
W_CHUNKS = tuple(slice(8 * i, 8 * i + 8) for i in range(3))


def kernel(
    ranges_h, board_h, targets_h, w_in_h, w_out_h,
    predicted_h, grad_in_h, grad_out_h, sums, loss,
    predicted, grad_in, grad_out, ranges, board, targets, w_in, w_out,
    stage, rows8, pack, weights, feats, grads_out,
    partial, rs_send, rs_long, rs_short, target_pad,
    hold, mine, cross, crossed, z_send, z_long, z_short, x_send, x_recv,
    ar_send, ar_zc, ar_xy, s_in, sent,
    r_wx, r_f, r_wz, r_wd, r_rs, r_gd, r_gx, r_ar,
):
    open_scope = []

    def mark(name):
        if PROFILE:
            if open_scope:
                open_scope.pop().__exit__(None, None, None)
            if name:
                open_scope.append(jax.named_scope(name))
                open_scope[-1].__enter__()

    mark("a_barrier")
    loads = [
        pltpu.make_async_copy(src, dst, s_in.at[i])
        for i, (src, dst) in enumerate(
            ((w_in_h, w_in), (w_out_h, w_out), (ranges_h, ranges), (board_h, board), (targets_h, targets))
        )
    ]
    for load in loads:
        load.start()
    d = lax.axis_index("dp")
    y = lax.axis_index("mp")
    c = lax.rem(d, 2)
    z = lax.rem(lax.div(d, 2), NZ)
    x = lax.div(d, 2 * NZ)
    sign = 1 - 2 * c
    me8 = x * 2 + c

    def around(base, step, n):
        return lax.rem(base + step + n, n)

    def at_dev(x_, z_, c_, y_):
        return {"dp": (x_ * NZ + z_) * 2 + c_, "mp": y_}

    def peer(k):
        return around(x, k // 2, NX), (c if k % 2 == 0 else 1 - c)

    def send(src, dst, s, r, device):
        copy = pltpu.make_async_remote_copy(
            src_ref=src, dst_ref=dst, send_sem=s, recv_sem=r, device_id=device, device_id_type=MESH
        )
        copy.start()
        return copy

    def wait_all(like, sem):
        pltpu.make_async_copy(like, like, sem).wait()

    y_long, y_short = around(y, sign, NY), around(y, -sign, NY)
    z_up, z_down = around(z, sign, NZ), around(z, -sign, NZ)
    to_y = (at_dev(x, z, c, y_long), at_dev(x, z, c, y_short))
    to_z = (at_dev(x, z_up, c, y), at_dev(x, z_down, c, y))
    partner = at_dev(x, z, 1 - c, y)

    barrier = pltpu.get_barrier_semaphore()
    near = [to_y[0], to_y[1], to_z[0], to_z[1]]
    for k in range(1, 8):
        px, pc = peer(k)
        near.append(at_dev(px, z, pc, y))
    for device in near:
        pl.semaphore_signal(barrier, inc=1, device_id=device, device_id_type=MESH)

    mark("b_stage")
    for i, (w, width) in enumerate(((w_in, INW), (w_out, OUTW))):
        loads[i].wait()
        stage[i, 0] = w[:, :HALF]
        stage[i, 1] = jnp.zeros((ROWS, HALF), BF16)
        stage[i, 1, :, : width - HALF] = w[:, HALF:]
    loads[2].wait()
    loads[3].wait()
    whole = OUTW // 128 * 128
    feats[0, y] = ranges[:, :HALF]
    feats[1, y, :, : whole - HALF] = ranges[:, HALF:whole]
    cards = lax.broadcasted_iota(jnp.int32, (256, STATES), 0) - (OUTW - whole)
    shown = jnp.zeros((256, STATES), F32)
    for k in range(5):
        shown = shown + (board[k : k + 1, :] == cards).astype(F32)
    diagonal = lax.broadcasted_iota(jnp.int32, (STATES, STATES), 0) == lax.broadcasted_iota(
        jnp.int32, (STATES, STATES), 1
    )
    shown = nt(diagonal.astype(F32).astype(BF16), shown.astype(BF16))
    tail = jnp.concatenate([ranges[:, whole:].astype(F32), jnp.zeros((STATES, whole + 256 - OUTW), F32)], axis=1)
    feats[1, y, :, whole - HALF :] = (tail + shown).astype(BF16)

    mark("c_barwait")
    pl.semaphore_wait(barrier, len(near))

    mark("d_xsend")
    for i in range(2):
        for k in range(1, 8):
            px, pc = peer(k)
            send(stage.at[i, pc], rows8.at[i, me8], sent.at[i], r_wx.at[i], at_dev(px, z, pc, y))

    def ring_gather(block_of, pos, n, to, s, r, arrived=lambda origin, j: None):
        copies = {}

        def step(k):
            for way, steps in ((0, LONG), (1, SHORT)):
                if k >= 1 and k - 1 < steps:
                    copies[way, k - 1].wait_recv()
                move = -k * sign if way == 0 else k * sign
                origin = around(pos, move, n)
                if k < steps:
                    block = block_of(origin)
                    copies[way, k] = send(block, block, s(way * LONG + k), r(way * LONG + k), to[way])
                if k >= 1 and k - 1 < steps:
                    arrived(origin, way * LONG + k)

        return step

    f_steps = [
        ring_gather(
            lambda o, p=p: feats.at[p[0], o, :, p[1]], y, NY, to_y,
            lambda j: sent.at[2], lambda j, q=q: r_f.at[q, j],
        )
        for q, p in enumerate(F_CHUNKS)
    ]
    for step in f_steps:
        step(0)
    for i in range(2):
        rows8[i, me8] = stage[i, c]
    loads[4].wait()
    target_pad[...] = jnp.zeros(target_pad.shape, F32)
    target_pad[0] = targets[:, :HALF].astype(F32)
    target_pad[1, :, : OUTW - HALF] = targets[:, HALF:].astype(F32)

    def to_partner(i, origin):
        block = weights.at[i, c, origin]
        send(block, block, sent.at[3 + i], r_wd.at[i], partner)

    mark("e_pack")
    w_steps = []
    for i in range(2):
        wait_all(rows8.at[i, 0:7], r_wx.at[i])
        for j in range(8):
            pack[i, ROWS * j : ROWS * (j + 1)] = rows8[i, j].astype(F32)
        weights[i, c, z] = pack[i].astype(BF16)
        w_steps.append([
            ring_gather(
                lambda o, i=i, p=p: weights.at[i, c, o, p], z, NZ, to_z,
                lambda j, i=i: sent.at[5 + i], lambda j, i=i, q=q: r_wz.at[i, q, j],
                (lambda o, j, i=i: to_partner(i, o)) if q == len(W_CHUNKS) - 1 else (lambda o, j: None),
            )
            for q, p in enumerate(W_CHUNKS)
        ])
        for step in w_steps[i]:
            step(0)
        to_partner(i, z)
    mark("f_ring1")
    for k in range(1, LONG + 1):
        for step in w_steps[0]:
            step(k)
        for step in f_steps:
            step(k)
        for step in w_steps[1]:
            step(k)
    mark("g_across")
    wait_all(weights.at[0, 1 - c], r_wd.at[0])

    def w_half(i, h):
        return weights[i, h].reshape(NZ * GROUP, HALF)

    def f_half(h):
        return feats[h].reshape(NY * STATES, HALF)

    mark("h_pre")
    pre = nt(w_half(0, 0), f_half(0)) + nt(w_half(0, 1), f_half(1))
    tanh = jnp.tanh(GELU_A * (pre + GELU_B * pre * pre * pre))
    hidden = 0.5 * pre * (1.0 + tanh)
    slope = 0.5 * (1.0 + tanh) + 0.5 * pre * (1.0 - tanh * tanh) * (GELU_A * (1.0 + 3.0 * GELU_B * pre * pre))
    hold[0] = hidden
    hold[1] = slope
    mark("i_partial")
    wait_all(weights.at[1, 1 - c], r_wd.at[1])
    hidden_t = hidden.T.astype(BF16)
    for h in range(2):
        partial[h] = nn(hidden_t, w_half(1, h)).reshape(NY, STATES, HALF)

    def ring_sum(term, pos, n, to, out, came, s, r):
        copies = {}

        def step(k):
            for way, steps in ((0, LONG), (1, SHORT)):
                if k < steps:
                    move = (steps - k) * sign if way == 0 else -(steps - k) * sign
                    value = term(around(pos, move, n))
                    if k >= 1:
                        copies[way, k - 1].wait_recv()
                        value = value + came(way, k - 1)[...].astype(F32)
                    j = way * LONG + k
                    out(j)[...] = value.astype(BF16)
                    copies[way, k] = send(out(j), came(way, k), s(j), r(j), to[way])

        def last():
            value = term(pos)
            for way, steps in ((1, SHORT), (0, LONG)):
                copies[way, steps - 1].wait_recv()
                value = value + came(way, steps - 1)[...].astype(F32)
            return value

        return step, last

    mark("j_rs")
    rs = [
        ring_sum(
            lambda t, p=p: partial[p[0], t, :, p[1]], y, NY, to_y, lambda j, p=p: rs_send.at[p[0], j, :, p[1]],
            lambda way, k, p=p: (rs_long, rs_short)[way].at[p[0], k, :, p[1]],
            lambda j, p=p: sent.at[7 + p[0]], lambda j, q=q: r_rs.at[q, j],
        )
        for q, p in enumerate(O_CHUNKS)
    ]
    for k in range(LONG):
        for step, last in rs:
            step(k)
    mark("k_loss")
    g_steps = []
    lost = jnp.zeros((1, 1), F32)
    for q, p in enumerate(O_CHUNKS):
        h, lanes = p
        summed = rs[q][1]()
        error = summed - target_pad[h, :, lanes]
        size = jnp.abs(error)
        grads_out[h, y, :, lanes] = jnp.clip(error, -1.0, 1.0).astype(BF16)
        g_steps.append(
            ring_gather(
                lambda o, p=p: grads_out.at[p[0], o, :, p[1]], y, NY, to_y,
                lambda j, p=p: sent.at[9 + p[0]], lambda j, q=q: r_f.at[q, j],
            )
        )
        g_steps[q](0)
        terms = jnp.where(size <= 1.0, 0.5 * error * error, size - 0.5)
        lost = lost + jnp.sum(terms, keepdims=True)
        left, right = h * HALF + lanes.start, min(h * HALF + lanes.stop, OUTW)
        predicted[:, left:right] = summed[:, : right - left].astype(BF16)
    stores = [pltpu.make_async_copy(predicted, predicted_h, s_in.at[5])]
    stores[0].start()
    grads_out[1, :, :, O_WIDTH - HALF :] = jnp.zeros((NY, STATES, 2 * HALF - O_WIDTH), BF16)
    mark("l_ag")
    for k in range(1, LONG + 1):
        for step in g_steps:
            step(k)

    def g_half(h):
        return grads_out[h].reshape(NY * STATES, HALF)

    def weight_grad(g, left, right):
        cross[g] = nn(left, right(1 - c)).astype(BF16).reshape(NZ, GROUP, HALF)
        copies = []
        for j, move in enumerate((4, -3, 3, -2, 2, -1, 1, 0)):
            t = around(z, -move * sign, NZ)
            copies.append(send(cross.at[g, t], crossed.at[g, t], sent.at[11 + g], r_gd.at[g, j], partner))
        mine[g] = nn(left, right(c)).reshape(NZ, GROUP, HALF)
        return copies

    def z_ring(g):
        return [
            ring_sum(
                lambda t, p=p: mine[g, t, p] + crossed[g, t, p].astype(F32), z, NZ, to_z,
                lambda j, p=p: z_send.at[g, j, p],
                lambda way, k, p=p: (z_long, z_short)[way].at[g, k, p],
                lambda j: sent.at[13 + g], lambda j, q=q: r_wz.at[g, q, j],
            )
            for q, p in enumerate(W_CHUNKS)
        ]

    mark("m_gout")
    over = {1: weight_grad(1, hold[0].astype(BF16), g_half)}
    mark("n_hgrad")
    hidden_grad = nt(w_half(1, 0), g_half(0)) + nt(w_half(1, 1), g_half(1))
    pre_grad = (hidden_grad * hold[1]).astype(BF16)
    mark("o_wait0")
    zr = {}

    def z_step(g, k):
        for j in ((0, 1), (2, 3), (4, 5), (6,), (7,))[k]:
            over[g][j].wait_recv()
        if k < LONG:
            for step, last in zr[g]:
                step(k)

    zr[1] = z_ring(1)
    z_step(1, 0)
    mark("p_gin")
    over[0] = weight_grad(0, pre_grad, f_half)
    mark("q_wait1")
    zr[0] = z_ring(0)
    z_step(0, 0)
    mark("r_zring")
    for k in range(1, LONG):
        z_step(1, k)
        z_step(0, k)
    mark("s_xsend")
    for g in (1, 0):
        z_step(g, LONG)
        for q, p in enumerate(W_CHUNKS):
            pack[g, p] = zr[g][q][1]()
        for j in range(8):
            x_send[g, j] = pack[g, ROWS * j : ROWS * (j + 1)].astype(BF16)
        for k in range(1, 8):
            px, pc = peer(k)
            send(x_send.at[g, px * 2 + pc], x_recv.at[g, me8], sent.at[15 + g], r_gx.at[g], at_dev(px, z, pc, y))
        x_recv[g, me8] = x_send[g, me8]
    mark("t_xrecv")
    squares = jnp.zeros((1, 1), F32)
    for g in (1, 0):
        wait_all(x_recv.at[g, 0:7], r_gx.at[g])
        for h in range(2):
            own = x_recv[g, h].astype(F32)
            for px in range(1, NX):
                own = own + x_recv[g, 2 * px + h].astype(F32)
            to = (grad_in, grad_out)[g]
            width = (INW, OUTW)[g]
            if h == 0:
                to[:, :HALF] = own
            else:
                own = own[:, : width - HALF]
                to[:, HALF:] = own
            squares = squares + jnp.sum(own * own, keepdims=True)
        stores.append(pltpu.make_async_copy(to, (grad_in_h, grad_out_h)[g], s_in.at[6 + g]))
        stores[-1].start()

    mark("u_ar")
    lane = lax.broadcasted_iota(jnp.int32, (1, 128), 1)
    total = jnp.where(lane == 0, squares, jnp.where(lane == 1, lost, 0.0))
    first = z * 2 + c
    ar_send[0] = total
    ar_zc[first] = total
    for k in range(1, 16):
        pz, pc = around(z, k // 2, NZ), (c if k % 2 == 0 else 1 - c)
        send(ar_send.at[0], ar_zc.at[first], sent.at[17], r_ar.at[0], at_dev(x, pz, pc, y))
    wait_all(ar_zc.at[0:15], r_ar.at[0])
    total = jnp.sum(ar_zc[...], axis=0)
    ar_send[1] = total
    second = x * NY + y
    ar_xy[second] = total
    for k in range(1, 32):
        send(
            ar_send.at[1], ar_xy.at[second], sent.at[18], r_ar.at[1],
            at_dev(around(x, k // NY, NX), z, c, around(y, k % NY, NY)),
        )
    wait_all(ar_xy.at[0:31], r_ar.at[1])
    total = jnp.sum(ar_xy[...], axis=0)
    sums[...] = total
    loss[...] = total[:, 1:2] / (BATCH * OUTW)
    mark("w_sends")
    for store in stores:
        store.wait()
    for i in range(2):
        wait_all(rows8.at[i, 0:7], sent.at[i])
        wait_all(weights.at[i, 0], sent.at[3 + i])
        wait_all(weights.at[i, 0, 0:7], sent.at[5 + i])
        wait_all(cross.at[i], sent.at[11 + i])
        wait_all(z_send.at[i], sent.at[13 + i])
        wait_all(x_send.at[i, 0:7], sent.at[15 + i])
        width = (HALF, O_WIDTH - HALF)[i]
        wait_all(rs_send.at[i, :, :, :width], sent.at[7 + i])
        wait_all(grads_out.at[i, 0:7, :, :width], sent.at[9 + i])
    wait_all(feats.at[:, 0:7], sent.at[2])
    wait_all(ar_zc.at[0:15], sent.at[17])
    wait_all(ar_xy.at[0:31], sent.at[18])
    mark(None)


def finish(
    predicted_i, grad_in_i, grad_out_i, sums_i, predicted_h, update_in_h, update_out_h,
    predicted, update_in, update_out, sums, r, s,
):
    loads = [
        pltpu.make_async_copy(src, dst, r.at[i])
        for i, (src, dst) in enumerate(
            ((sums_i, sums), (predicted_i, predicted), (grad_in_i, update_in), (grad_out_i, update_out))
        )
    ]
    stores = [
        pltpu.make_async_copy(src, dst, s.at[i])
        for i, (src, dst) in enumerate(
            ((predicted, predicted_h), (update_in, update_in_h), (update_out, update_out_h))
        )
    ]
    for load in loads:
        load.start()
    loads[1].wait()
    stores[0].start()
    loads[0].wait()
    scale = lax.rsqrt(sums[:, 0:1] / (HIDDEN * (INW + OUTW)) + 1e-6)
    for i, update in ((1, update_in), (2, update_out)):
        loads[i + 1].wait()
        update[...] = update[...] * scale
        stores[i].start()
    for store in stores:
        store.wait()


def body(ranges, board, targets, w_in, w_out):
    vmem = pl.BlockSpec(memory_space=pltpu.VMEM)
    hbm = pl.BlockSpec(memory_space=pltpu.HBM)
    dma = pltpu.SemaphoreType.DMA
    scratch = [
        pltpu.VMEM((STATES, OUTW), BF16),
        pltpu.VMEM((ROWS, INW), F32),
        pltpu.VMEM((ROWS, OUTW), F32),
        pltpu.VMEM((STATES, OUTW), BF16),
        pltpu.VMEM((5, STATES), jnp.int32),
        pltpu.VMEM((STATES, OUTW), BF16),
        pltpu.VMEM((ROWS, INW), BF16),
        pltpu.VMEM((ROWS, OUTW), BF16),
        pltpu.VMEM((2, 2, ROWS, HALF), BF16),
        pltpu.VMEM((2, 8, ROWS, HALF), BF16),
        pltpu.VMEM((2, GROUP, HALF), F32),
        pltpu.VMEM((2, 2, NZ, GROUP, HALF), BF16),
        pltpu.VMEM((2, NY, STATES, HALF), BF16),
        pltpu.VMEM((2, NY, STATES, HALF), BF16),
        pltpu.VMEM((2, NY, STATES, HALF), F32),
        pltpu.VMEM((2, 7, STATES, HALF), BF16),
        pltpu.VMEM((2, LONG, STATES, HALF), BF16),
        pltpu.VMEM((2, SHORT, STATES, HALF), BF16),
        pltpu.VMEM((2, STATES, HALF), F32),
        pltpu.VMEM((2, NZ * GROUP, NY * STATES), F32),
        pltpu.VMEM((2, NZ, GROUP, HALF), F32),
        pltpu.VMEM((2, NZ, GROUP, HALF), BF16),
        pltpu.VMEM((2, NZ, GROUP, HALF), BF16),
        pltpu.VMEM((2, 7, GROUP, HALF), BF16),
        pltpu.VMEM((2, LONG, GROUP, HALF), BF16),
        pltpu.VMEM((2, SHORT, GROUP, HALF), BF16),
        pltpu.VMEM((2, 8, ROWS, HALF), BF16),
        pltpu.VMEM((2, 8, ROWS, HALF), BF16),
        pltpu.VMEM((2, 1, 128), F32),
        pltpu.VMEM((16, 1, 128), F32),
        pltpu.VMEM((32, 1, 128), F32),
        dma((8,)),
        dma((19,)),
    ]
    for shape in ((2,), (len(F_CHUNKS), 7), (2, len(W_CHUNKS), 7), (2,), (len(O_CHUNKS), 7), (2, 8), (2,), (2,)):
        scratch.append(dma(shape))
    made = (
        jax.ShapeDtypeStruct((STATES, OUTW), BF16),
        jax.ShapeDtypeStruct((ROWS, INW), F32),
        jax.ShapeDtypeStruct((ROWS, OUTW), F32),
        jax.ShapeDtypeStruct((1, 128), F32),
        jax.ShapeDtypeStruct((1, 1), F32),
    )
    made = pl.pallas_call(
        kernel,
        name="step",
        out_shape=made,
        in_specs=[hbm] * 5,
        out_specs=(hbm, hbm, hbm, vmem, vmem),
        scratch_shapes=scratch,
        compiler_params=pltpu.CompilerParams(
            collective_id=0, has_side_effects=True, vmem_limit_bytes=VMEM_STEP
        ),
    )(ranges, board.T, targets, w_in, w_out)
    outs = (
        jax.ShapeDtypeStruct((STATES, OUTW), BF16),
        jax.ShapeDtypeStruct((ROWS, INW), F32),
        jax.ShapeDtypeStruct((ROWS, OUTW), F32),
    )
    outs = pl.pallas_call(
        finish,
        name="finish",
        out_shape=outs,
        in_specs=[hbm] * 4,
        out_specs=(hbm,) * 3,
        scratch_shapes=[
            pltpu.VMEM((STATES, OUTW), BF16),
            pltpu.VMEM((ROWS, INW), F32),
            pltpu.VMEM((ROWS, OUTW), F32),
            pltpu.VMEM((1, 128), F32),
            dma((4,)),
            dma((3,)),
        ],
        compiler_params=pltpu.CompilerParams(vmem_limit_bytes=VMEM_STEP),
    )(*made[:4])
    return outs[0], outs[1], outs[2], made[4][0, 0]


def solution(mesh):
    rows, units = P(("dp", "mp"), None), P(("mp", "dp"), None)
    return jax.shard_map(
        body,
        mesh=mesh,
        in_specs=(rows, rows, rows, units, units),
        out_specs=(rows, units, units, P()),
        check_vma=False,
    )
```

time: 109 us -> 98.1 us (0.90)
  local copies, waits for them, and re-layouts: 5.88 us -> 0 us
  Pallas kernels: 100 us -> 95.5 us
    unnamed x12 -> x0, local copies, waits for them, and re-layouts: 5.88 us -> none
    pallas_call x1 -> x2, Pallas kernels: 100 us -> 95.5 us  [the longest x1 93.8 us: body(): pl.pallas_call(kernel, name='step', out_shape=made, in_specs=[hbm] * 5, o...]
where the time goes in v2:
time: 98.1 us; the launch traced here: 97.9 us
  Pallas kernels  95.5 us (97%)
  between operations  2.4 us (2%)
    pallas_call x1, Pallas kernels, body(): pl.pallas_call(kernel, name='step', out_shape=made, in_specs=[hbm] * 5, o...  93.8 us

profile of v2, /device:TPU:1, one launch (start us, length us, event | category | flops | bytes accessed | tf_op | source)
XLA Modules:
  0.0 97.9 jit_solution(17141539913920344990)
XLA Ops:
  0.6 93.8 %step.1 = (bf16[16,2652]{1,0:T(8,128)(2,1)}, f32[3,2704]{1,0:T(4,128)}, f32[3,2652]{1,0:T(4,128)}, f32[1,128]{1,0:T(1,128)}, f32[1,1]{1,0:T(1,128)}) custom-call(bf16[16,2652]{1,0:T(8,128)(2,1)} %ranges_h.1, s32[5,16]{1,0:T(8,128)} %bitcast.2, bf16[16,2652]{1,0:T(8,128)(2,1)} %targets_h.1, bf16[3,2704]{1,0:T(4,128)(2,1)} %w_in_h.1, bf16[3,2652]{1,0:T(4,128)(2,1)} %w_out_h.1), custom_call_target="tpu_custom_call" | custom-call | tf_op jit(solution)/shard_map/step/pallas_call | solution.py:487
  94.5 1.7 %finish.1 = (bf16[16,2652]{1,0:T(8,128)(2,1)}, f32[3,2704]{1,0:T(4,128)}, f32[3,2652]{1,0:T(4,128)}) custom-call(bf16[16,2652]{1,0:T(8,128)(2,1)} %get-tuple-element.12.predicted_i, f32[3,2704]{1,0:T(4,128)} %get-tuple-element.13.grad_in_i, f32[3,2652]{1,0:T(4,128)} %get-tuple-element.14.grad_out_i, f32[1,128]{1,0:T(1,128)} %get-tuple-element.15.sums_i), custom_call_target="tpu_custom_call" | custom-call | tf_op jit(solution)/shard_map/finish/pallas_call | solution.py:503

commit v3 on v2

v3 whole, which is shorter than its diff:
```python
import jax
import jax.numpy as jnp
from jax import lax
from jax.experimental import pallas as pl
from jax.experimental.pallas import tpu as pltpu
from jax.sharding import PartitionSpec as P

PROFILE = False
VMEM_STEP = 67043328
MESH = pl.DeviceIdType.MESH
BF16, F32 = jnp.bfloat16, jnp.float32
NX, NZ, NY = 4, 8, 8
ROWS, LINE, STATES = 3, 24, 16
INW, OUTW, HIDDEN, BATCH = 2704, 2652, 1536, 8192
WIDE, WIDE_OUT = 2816, 2688
LONG, SHORT = 4, 3
GELU_A, GELU_B = 0.7978845608028654, 0.044715
O_CHUNKS = tuple(slice(128 * a, 128 * b) for a, b in ((0, 6), (6, 11), (11, 16), (16, 21)))
W_CHUNKS = tuple(
    tuple((slice(8 * i, 8 * i + 8), slice(a, b)) for i in range(3) for a, b in ((0, 1408), (1408, width)))
    for width in (WIDE, WIDE_OUT)
)


def nt(a, b):
    return lax.dot_general(a, b, (((1,), (1,)), ((), ())), preferred_element_type=F32)


def nn(a, b):
    return lax.dot_general(a, b, (((1,), (0,)), ((), ())), preferred_element_type=F32)


def kernel(
    ranges_h, board_h, targets_h, w_in_h, w_out_h,
    predicted_h, grad_in_h, grad_out_h, sums, loss,
    predicted, grad_in, grad_out, ranges, board, targets, w_in, w_out,
    stage, rows8, pack, weights, feats, values_grad, hidden_t, partial, cross, crossed, to_x, from_x,
    target_pad, hold, order, mine, ring_send, ring_long, ring_short, line_send, line_recv,
    ar_send, ar_zc, ar_xy, s_in, sent,
    r_w, r_ring, r_f, r_cross, r_sum, r_grad, r_line, r_ar,
):
    open_scope = []

    def mark(name):
        if PROFILE:
            if open_scope:
                open_scope.pop().__exit__(None, None, None)
            if name:
                open_scope.append(jax.named_scope(name))
                open_scope[-1].__enter__()

    mark("a_barrier")
    loads = [
        pltpu.make_async_copy(src, dst, s_in.at[i])
        for i, (src, dst) in enumerate(
            ((w_in_h, w_in), (w_out_h, w_out), (ranges_h, ranges), (board_h, board), (targets_h, targets))
        )
    ]
    for load in loads:
        load.start()
    d = lax.axis_index("dp")
    y = lax.axis_index("mp")
    c = lax.rem(d, 2)
    z = lax.rem(lax.div(d, 2), NZ)
    x = lax.div(d, 2 * NZ)
    sign = 1 - 2 * c

    def around(base, step, n):
        return lax.rem(base + step + n, n)

    def at_dev(x_, z_, c_, y_):
        return {"dp": (x_ * NZ + z_) * 2 + c_, "mp": y_}

    def x_peer(k):
        return at_dev(around(x, k, NX), z, c, y)

    def y_peer(k):
        return at_dev(x, z, c, around(y, k, NY))

    def z_peer(k):
        return at_dev(x, around(z, k, NZ), c, y)

    partner = at_dev(x, z, 1 - c, y)

    def send(src, dst, s, r, device):
        copy = pltpu.make_async_remote_copy(
            src_ref=src, dst_ref=dst, send_sem=s, recv_sem=r, device_id=device, device_id_type=MESH
        )
        copy.start()
        return copy

    def wait_all(like, sem):
        pltpu.make_async_copy(like, like, sem).wait()

    barrier = pltpu.get_barrier_semaphore()
    near = [y_peer(k) for k in range(1, NY)] + [z_peer(k) for k in range(1, NZ)]
    near += [x_peer(k) for k in range(1, NX)] + [partner]
    for device in near:
        pl.semaphore_signal(barrier, inc=1, device_id=device, device_id_type=MESH)

    mark("b_stage")
    whole = OUTW // 128 * 128
    for i, (w, width) in enumerate(((w_in, INW), (w_out, OUTW))):
        loads[i].wait()
        stage[i, :, whole:] = jnp.zeros((ROWS, WIDE - whole), BF16)
        stage[i, :, :width] = w[...]
    loads[2].wait()
    loads[3].wait()
    feats[c, x, :, :whole] = ranges[:, :whole]
    cards = lax.broadcasted_iota(jnp.int32, (WIDE - whole, STATES), 0) - (OUTW - whole)
    shown = jnp.zeros((WIDE - whole, STATES), F32)
    for k in range(5):
        shown = shown + (board[k : k + 1, :] == cards).astype(F32)
    diagonal = lax.broadcasted_iota(jnp.int32, (STATES, STATES), 0) == lax.broadcasted_iota(
        jnp.int32, (STATES, STATES), 1
    )
    shown = nt(diagonal.astype(F32).astype(BF16), shown.astype(BF16))
    tail = jnp.concatenate([ranges[:, whole:].astype(F32), jnp.zeros((STATES, WIDE - OUTW), F32)], axis=1)
    feats[c, x, :, whole:] = (tail + shown).astype(BF16)

    mark("c_barwait")
    pl.semaphore_wait(barrier, len(near))

    mark("d_xsend")
    line = ((y, NY, y_peer), (z, NZ, z_peer))
    ring = ((z, NZ, (z_peer(sign), z_peer(-sign))), (y, NY, (y_peer(sign), y_peer(-sign))))
    for i in range(2):
        pos, n, peer = line[i]
        for k in (1, 7, 2, 6, 3, 5, 4):
            send(stage.at[i], rows8.at[i, pos], sent.at[i], r_w.at[i], peer(k))
    for k in range(1, NX):
        send(feats.at[c, x], feats.at[c, x], sent.at[2], r_f.at[0], x_peer(k))
    for i in range(2):
        rows8[i, line[i][0]] = stage[i]
    loads[4].wait()
    target_pad[:, :OUTW] = targets[...].astype(F32)
    target_pad[:, whole:] = jnp.concatenate(
        [targets[:, whole:].astype(F32), jnp.zeros((STATES, WIDE_OUT - OUTW), F32)], axis=1
    )

    def ring_gather(block_of, i, r):
        pos, n, to = ring[i]
        copies = {}

        def step(k):
            for way, steps in ((0, LONG), (1, SHORT)):
                if k >= 1 and k - 1 < steps:
                    copies[way, k - 1].wait_recv()
                if k < steps:
                    block = block_of(around(pos, -k * sign if way == 0 else k * sign, n))
                    copies[way, k] = send(block, block, sent.at[4 + i], r(way * LONG + k), to[way])

        return step

    mark("e_pack")
    w_steps = []
    for i in range(2):
        wait_all(rows8.at[i, 0:7], r_w.at[i])
        for j in range(8):
            pack[i, ROWS * j : ROWS * (j + 1)] = rows8[i, j].astype(F32)
        weights[i, ring[i][0]] = pack[i].astype(BF16)
        w_steps.append(
            [
                ring_gather(lambda o, i=i, p=p: weights.at[i, o, p[0], p[1]], i, lambda j, i=i, q=q: r_ring.at[i, q, j])
                for q, p in enumerate(W_CHUNKS[i])
            ]
        )
        for step in w_steps[i]:
            step(0)
    mark("f_ring1")
    wait_all(feats.at[0, 0:3], r_f.at[0])
    send(feats.at[c], feats.at[c], sent.at[3], r_f.at[1], partner)
    for k in range(1, LONG + 1):
        for steps in zip(*w_steps):
            for step in steps:
                step(k)
    mark("g_across")
    wait_all(feats.at[1 - c], r_f.at[1])

    def units(i):
        if i == 0:
            return weights[0].reshape(NZ * LINE, WIDE)
        return weights[1, :, :, :WIDE_OUT].reshape(NY * LINE, WIDE_OUT)

    def states(ref, width):
        return ref[:, :, :, :width].reshape(2 * NX * STATES, width)

    def reorder(src, dst):
        for a in range(8):
            for b in range(8):
                dst[b, ROWS * a : ROWS * (a + 1)] = src[a, ROWS * b : ROWS * (b + 1)]

    mark("h_pre")
    order[0] = nt(units(0), states(feats, WIDE)).reshape(NZ, LINE, 2 * NX * STATES)
    reorder(order.at[0], order.at[1])
    pre = order[1].reshape(NY * LINE, 2 * NX * STATES)
    tanh = jnp.tanh(GELU_A * (pre + GELU_B * pre * pre * pre))
    hidden = 0.5 * pre * (1.0 + tanh)
    slope = 0.5 * (1.0 + tanh) + 0.5 * pre * (1.0 - tanh * tanh) * (GELU_A * (1.0 + 3.0 * GELU_B * pre * pre))
    hold[0] = hidden
    hold[1] = slope
    hidden_t[...] = hidden.T.astype(BF16).reshape(2, NX * STATES, NY * LINE)

    mark("i_partial")
    cross[...] = nn(hidden_t[1 - c], units(1)).astype(BF16).reshape(NX, STATES, WIDE_OUT)
    for q, p in enumerate(O_CHUNKS):
        send(cross.at[:, :, p], crossed.at[:, :, p], sent.at[6], r_cross.at[q], partner)
    partial[...] = nn(hidden_t[c], units(1)).reshape(NX, STATES, WIDE_OUT)
    mark("j_rs")
    for q, p in enumerate(O_CHUNKS):
        wait_all(crossed.at[:, :, p], r_cross.at[q])
        for k in (2, 1, 3):
            px = around(x, k, NX)
            to_x[px, :, p] = (partial[px, :, p] + crossed[px, :, p].astype(F32)).astype(BF16)
            send(to_x.at[px, :, p], from_x.at[x, :, p], sent.at[7], r_sum.at[q], x_peer(k))
    mark("k_loss")
    lost = jnp.zeros((1, 1), F32)
    for q, p in enumerate(O_CHUNKS):
        wait_all(from_x.at[0:3, :, p], r_sum.at[q])
        summed = partial[x, :, p] + crossed[x, :, p].astype(F32)
        for k in range(1, NX):
            summed = summed + from_x[around(x, k, NX), :, p].astype(F32)
        error = summed - target_pad[:, p]
        values_grad[c, x, :, p] = jnp.clip(error, -1.0, 1.0).astype(BF16)
        for k in (2, 1, 3):
            block = values_grad.at[c, x, :, p]
            send(block, block, sent.at[8], r_grad.at[q], x_peer(k))
        size = jnp.abs(error)
        terms = jnp.where(size <= 1.0, 0.5 * error * error, size - 0.5)
        lost = lost + jnp.sum(terms, keepdims=True)
        right = min(p.stop, OUTW)
        predicted[:, p.start : right] = summed[:, : right - p.start].astype(BF16)
    stores = [pltpu.make_async_copy(predicted, predicted_h, s_in.at[5])]
    stores[0].start()
    mark("l_ag")
    for q, p in enumerate(O_CHUNKS):
        wait_all(from_x.at[0:3, :, p], r_grad.at[q])
        block = values_grad.at[c, :, :, p]
        send(block, block, sent.at[9], r_cross.at[4], partner)
    wait_all(values_grad.at[1 - c, :, :, :WIDE_OUT], r_cross.at[4])

    def ring_sum(g, q, p):
        pos, n, to = ring[g]
        copies = {}

        def came(way, k):
            return (ring_long, ring_short)[way].at[g, k, p[0], p[1]]

        def term(t):
            return mine[g, t, p[0], p[1]]

        def step(k):
            for way, steps in ((0, LONG), (1, SHORT)):
                if k < steps:
                    move = (steps - k) * sign if way == 0 else -(steps - k) * sign
                    value = term(around(pos, move, n))
                    if k >= 1:
                        copies[way, k - 1].wait_recv()
                        value = value + came(way, k - 1)[...].astype(F32)
                    j = way * LONG + k
                    out = ring_send.at[g, j, p[0], p[1]]
                    out[...] = value.astype(BF16)
                    copies[way, k] = send(out, came(way, k), sent.at[10 + g], r_ring.at[g, q, j], to[way])

        def last():
            value = term(pos)
            for way, steps in ((1, SHORT), (0, LONG)):
                copies[way, steps - 1].wait_recv()
                value = value + came(way, steps - 1)[...].astype(F32)
            return value

        return step, last

    mark("m_gout")
    sums_of = {g: [ring_sum(g, q, p) for q, p in enumerate(W_CHUNKS[g])] for g in (1, 0)}
    mine[1, :, :, :WIDE_OUT] = nn(hold[0].astype(BF16), states(values_grad, WIDE_OUT)).reshape(NY, LINE, WIDE_OUT)
    for step, last in sums_of[1]:
        step(0)
    mark("n_hgrad")
    hidden_grad = nt(units(1), states(values_grad, WIDE_OUT))
    order[1] = (hidden_grad * hold[1]).reshape(NY, LINE, 2 * NX * STATES)
    reorder(order.at[1], order.at[0])
    pre_grad = order[0].reshape(NZ * LINE, 2 * NX * STATES).astype(BF16)
    mark("p_gin")
    mine[0] = nn(pre_grad, states(feats, WIDE)).reshape(NZ, LINE, WIDE)
    for step, last in sums_of[0]:
        step(0)
    mark("r_zring")
    for k in range(1, LONG):
        for g in (1, 0):
            for step, last in sums_of[g]:
                step(k)
    mark("s_xsend")
    for g in (1, 0):
        pos, n, peer = line[g]
        for q, p in enumerate(W_CHUNKS[g]):
            pack[g, p[0], p[1]] = sums_of[g][q][1]()
        for j in range(8):
            line_send[g, j] = pack[g, ROWS * j : ROWS * (j + 1)].astype(BF16)
        for k in (4, 3, 5, 2, 6, 1, 7):
            send(line_send.at[g, around(pos, k, n)], line_recv.at[g, pos], sent.at[12 + g], r_line.at[g], peer(k))
        line_recv[g, pos] = line_send[g, pos]
    mark("t_xrecv")
    squares = jnp.zeros((1, 1), F32)
    for g in (1, 0):
        to, width = ((grad_in, INW), (grad_out, OUTW))[g]
        wait_all(line_recv.at[g, 0:7], r_line.at[g])
        own = line_recv[g, 0].astype(F32)
        for j in range(1, 8):
            own = own + line_recv[g, j].astype(F32)
        own = own[:, :width]
        to[...] = own
        stores.append(pltpu.make_async_copy(to, (grad_in_h, grad_out_h)[g], s_in.at[6 + g]))
        stores[-1].start()
        squares = squares + jnp.sum(own * own, keepdims=True)

    mark("u_ar")
    lane = lax.broadcasted_iota(jnp.int32, (1, 128), 1)
    total = jnp.where(lane == 0, squares, jnp.where(lane == 1, lost, 0.0))
    first = z * 2 + c
    ar_send[0] = total
    ar_zc[first] = total
    for k in range(1, 16):
        pz, pc = around(z, k // 2, NZ), (c if k % 2 == 0 else 1 - c)
        send(ar_send.at[0], ar_zc.at[first], sent.at[14], r_ar.at[0], at_dev(x, pz, pc, y))
    wait_all(ar_zc.at[0:15], r_ar.at[0])
    total = jnp.sum(ar_zc[...], axis=0)
    ar_send[1] = total
    second = x * NY + y
    ar_xy[second] = total
    for k in range(1, 32):
        send(
            ar_send.at[1], ar_xy.at[second], sent.at[15], r_ar.at[1],
            at_dev(around(x, k // NY, NX), z, c, around(y, k % NY, NY)),
        )
    wait_all(ar_xy.at[0:31], r_ar.at[1])
    total = jnp.sum(ar_xy[...], axis=0)
    sums[...] = total
    loss[...] = total[:, 1:2] / (BATCH * OUTW)
    mark("w_sends")
    for store in stores:
        store.wait()
    for i in range(2):
        wait_all(rows8.at[i, 0:7], sent.at[i])
        wait_all(weights.at[i, 0:7, :, : (WIDE, WIDE_OUT)[i]], sent.at[4 + i])
        wait_all(ring_send.at[i, :, :, : (WIDE, WIDE_OUT)[i]], sent.at[10 + i])
        wait_all(line_send.at[i, 0:7], sent.at[12 + i])
    wait_all(feats.at[0, 0:3], sent.at[2])
    wait_all(feats.at[0], sent.at[3])
    wait_all(cross, sent.at[6])
    wait_all(to_x.at[0:3], sent.at[7])
    wait_all(to_x.at[0:3], sent.at[8])
    wait_all(cross, sent.at[9])
    wait_all(ar_zc.at[0:15], sent.at[14])
    wait_all(ar_xy.at[0:31], sent.at[15])
    mark(None)


def finish(
    predicted_i, grad_in_i, grad_out_i, sums_i, predicted_h, update_in_h, update_out_h,
    predicted, update_in, update_out, sums, r, s,
):
    loads = [
        pltpu.make_async_copy(src, dst, r.at[i])
        for i, (src, dst) in enumerate(
            ((sums_i, sums), (predicted_i, predicted), (grad_in_i, update_in), (grad_out_i, update_out))
        )
    ]
    stores = [
        pltpu.make_async_copy(src, dst, s.at[i])
        for i, (src, dst) in enumerate(
            ((predicted, predicted_h), (update_in, update_in_h), (update_out, update_out_h))
        )
    ]
    for load in loads:
        load.start()
    loads[1].wait()
    stores[0].start()
    loads[0].wait()
    scale = lax.rsqrt(sums[:, 0:1] / (HIDDEN * (INW + OUTW)) + 1e-6)
    for i, update in ((1, update_in), (2, update_out)):
        loads[i + 1].wait()
        update[...] = update[...] * scale
        stores[i].start()
    for store in stores:
        store.wait()


def body(ranges, board, targets, w_in, w_out):
    vmem = pl.BlockSpec(memory_space=pltpu.VMEM)
    hbm = pl.BlockSpec(memory_space=pltpu.HBM)
    dma = pltpu.SemaphoreType.DMA
    scratch = [
        pltpu.VMEM((STATES, OUTW), BF16),
        pltpu.VMEM((ROWS, INW), F32),
        pltpu.VMEM((ROWS, OUTW), F32),
        pltpu.VMEM((STATES, OUTW), BF16),
        pltpu.VMEM((5, STATES), jnp.int32),
        pltpu.VMEM((STATES, OUTW), BF16),
        pltpu.VMEM((ROWS, INW), BF16),
        pltpu.VMEM((ROWS, OUTW), BF16),
        pltpu.VMEM((2, ROWS, WIDE), BF16),
        pltpu.VMEM((2, 8, ROWS, WIDE), BF16),
        pltpu.VMEM((2, LINE, WIDE), F32),
        pltpu.VMEM((2, 8, LINE, WIDE), BF16),
        pltpu.VMEM((2, NX, STATES, WIDE), BF16),
        pltpu.VMEM((2, NX, STATES, WIDE), BF16),
        pltpu.VMEM((2, NX * STATES, 8 * LINE), BF16),
        pltpu.VMEM((NX, STATES, WIDE_OUT), F32),
        pltpu.VMEM((NX, STATES, WIDE_OUT), BF16),
        pltpu.VMEM((NX, STATES, WIDE_OUT), BF16),
        pltpu.VMEM((NX, STATES, WIDE_OUT), BF16),
        pltpu.VMEM((NX, STATES, WIDE_OUT), BF16),
        pltpu.VMEM((STATES, WIDE_OUT), F32),
        pltpu.VMEM((2, 8 * LINE, 2 * NX * STATES), F32),
        pltpu.VMEM((2, 8, LINE, 2 * NX * STATES), F32),
        pltpu.VMEM((2, 8, LINE, WIDE), F32),
        pltpu.VMEM((2, 7, LINE, WIDE), BF16),
        pltpu.VMEM((2, LONG, LINE, WIDE), BF16),
        pltpu.VMEM((2, SHORT, LINE, WIDE), BF16),
        pltpu.VMEM((2, 8, ROWS, WIDE), BF16),
        pltpu.VMEM((2, 8, ROWS, WIDE), BF16),
        pltpu.VMEM((2, 1, 128), F32),
        pltpu.VMEM((16, 1, 128), F32),
        pltpu.VMEM((32, 1, 128), F32),
        dma((8,)),
        dma((16,)),
    ]
    for shape in ((2,), (2, 6, 7), (2,), (5,), (4,), (4,), (2,), (2,)):
        scratch.append(dma(shape))
    made = (
        jax.ShapeDtypeStruct((STATES, OUTW), BF16),
        jax.ShapeDtypeStruct((ROWS, INW), F32),
        jax.ShapeDtypeStruct((ROWS, OUTW), F32),
        jax.ShapeDtypeStruct((1, 128), F32),
        jax.ShapeDtypeStruct((1, 1), F32),
    )
    made = pl.pallas_call(
        kernel,
        name="step",
        out_shape=made,
        in_specs=[hbm] * 5,
        out_specs=(hbm, hbm, hbm, vmem, vmem),
        scratch_shapes=scratch,
        compiler_params=pltpu.CompilerParams(
            collective_id=0, has_side_effects=True, vmem_limit_bytes=VMEM_STEP
        ),
    )(ranges, board.T, targets, w_in, w_out)
    outs = (
        jax.ShapeDtypeStruct((STATES, OUTW), BF16),
        jax.ShapeDtypeStruct((ROWS, INW), F32),
        jax.ShapeDtypeStruct((ROWS, OUTW), F32),
    )
    outs = pl.pallas_call(
        finish,
        name="finish",
        out_shape=outs,
        in_specs=[hbm] * 4,
        out_specs=(hbm,) * 3,
        scratch_shapes=[
            pltpu.VMEM((STATES, OUTW), BF16),
            pltpu.VMEM((ROWS, INW), F32),
            pltpu.VMEM((ROWS, OUTW), F32),
            pltpu.VMEM((1, 128), F32),
            dma((4,)),
            dma((3,)),
        ],
        compiler_params=pltpu.CompilerParams(vmem_limit_bytes=VMEM_STEP),
    )(*made[:4])
    return outs[0], outs[1], outs[2], made[4][0, 0]


def solution(mesh):
    rows, units = P(("dp", "mp"), None), P(("mp", "dp"), None)
    return jax.shard_map(
        body,
        mesh=mesh,
        in_specs=(rows, rows, rows, units, units),
        out_specs=(rows, units, units, P()),
        check_vma=False,
    )
```

time: 98.1 us -> 93.3 us (0.951)
  Pallas kernels: 95.5 us -> 90.7 us
    pallas_call x1, Pallas kernels: 93.8 us -> 89 us  [body(): pl.pallas_call(kernel, name='step', out_shape=made, in_specs=[hbm] * 5, o...]
where the time goes in v3:
time: 93.3 us; the launch traced here: 93.1 us
  Pallas kernels  90.7 us (97%)
  between operations  2.4 us (3%)
    pallas_call x1, Pallas kernels, body(): pl.pallas_call(kernel, name='step', out_shape=made, in_specs=[hbm] * 5, o...  89 us

profile of v3, /device:TPU:1, one launch (start us, length us, event | category | flops | bytes accessed | tf_op | source)
XLA Modules:
  0.0 93.1 jit_solution(10283526086823956679)
XLA Ops:
  0.6 89.0 %step.1 = (bf16[16,2652]{1,0:T(8,128)(2,1)}, f32[3,2704]{1,0:T(4,128)}, f32[3,2652]{1,0:T(4,128)}, f32[1,128]{1,0:T(1,128)}, f32[1,1]{1,0:T(1,128)}) custom-call(bf16[16,2652]{1,0:T(8,128)(2,1)} %ranges_h.1, s32[5,16]{1,0:T(8,128)} %bitcast.2, bf16[16,2652]{1,0:T(8,128)(2,1)} %targets_h.1, bf16[3,2704]{1,0:T(4,128)(2,1)} %w_in_h.1, bf16[3,2652]{1,0:T(4,128)(2,1)} %w_out_h.1), custom_call_target="tpu_custom_call" | custom-call | tf_op jit(solution)/shard_map/step/pallas_call | solution.py:438
  89.6 1.7 %finish.1 = (bf16[16,2652]{1,0:T(8,128)(2,1)}, f32[3,2704]{1,0:T(4,128)}, f32[3,2652]{1,0:T(4,128)}) custom-call(bf16[16,2652]{1,0:T(8,128)(2,1)} %get-tuple-element.12.predicted_i, f32[3,2704]{1,0:T(4,128)} %get-tuple-element.13.grad_in_i, f32[3,2652]{1,0:T(4,128)} %get-tuple-element.14.grad_out_i, f32[1,128]{1,0:T(1,128)} %get-tuple-element.15.sums_i), custom_call_target="tpu_custom_call" | custom-call | tf_op jit(solution)/shard_map/finish/pallas_call | solution.py:454

commit v4 on v3

--- a/solution.py
+++ b/solution.py
@@ -12,16 +12,23 @@
 NX, NZ, NY = 4, 8, 8
 ROWS, LINE, STATES = 3, 24, 16
 INW, OUTW, HIDDEN, BATCH = 2704, 2652, 1536, 8192
-WIDE, WIDE_OUT = 2816, 2688
+WIDE, WIDE_OUT, HALF = 2816, 2688, 1408
+SPLIT, PACKED = 768, 2176
 LONG, SHORT = 4, 3
+FAR_FIRST = (4, 3, 5, 2, 6, 1, 7)
 GELU_A, GELU_B = 0.7978845608028654, 0.044715
 O_CHUNKS = tuple(slice(128 * a, 128 * b) for a, b in ((0, 6), (6, 11), (11, 16), (16, 21)))
 W_CHUNKS = tuple(
-    tuple((slice(8 * i, 8 * i + 8), slice(a, b)) for i in range(3) for a, b in ((0, 1408), (1408, width)))
+    tuple((slice(8 * i, 8 * i + 8), slice(a, b)) for a, b in ((0, HALF), (HALF, width)) for i in range(3))
     for width in (WIDE, WIDE_OUT)
 )
 
 
+def fold(rows):
+    third = jnp.concatenate([rows[2:3, SPLIT:], jnp.zeros((1, PACKED - 2 * HALF + SPLIT), F32)], axis=1)
+    return rows[0:2].astype(BF16), jnp.concatenate([rows[2:3, :SPLIT], third], axis=0).astype(BF16)
+
+
 def nt(a, b):
     return lax.dot_general(a, b, (((1,), (1,)), ((), ())), preferred_element_type=F32)
 
@@ -32,8 +39,8 @@
 
 def kernel(
     ranges_h, board_h, targets_h, w_in_h, w_out_h,
-    predicted_h, grad_in_h, grad_out_h, sums, loss,
-    predicted, grad_in, grad_out, ranges, board, targets, w_in, w_out,
+    predicted_h, grad_in_h, grad_out_h, sums_h,
+    predicted, grad_in, grad_out, sums, ranges, board, targets, w_in, w_out,
     stage, rows8, pack, weights, feats, values_grad, hidden_t, partial, cross, crossed, to_x, from_x,
     target_pad, hold, order, mine, ring_send, ring_long, ring_short, line_send, line_recv,
     ar_send, ar_zc, ar_xy, s_in, sent,
@@ -102,8 +109,10 @@
     whole = OUTW // 128 * 128
     for i, (w, width) in enumerate(((w_in, INW), (w_out, OUTW))):
         loads[i].wait()
-        stage[i, :, whole:] = jnp.zeros((ROWS, WIDE - whole), BF16)
-        stage[i, :, :width] = w[...]
+        left = w[:, :HALF].astype(F32)
+        right = jnp.concatenate([w[:, HALF:].astype(F32), jnp.zeros((ROWS, WIDE - width), F32)], axis=1)
+        for h, rows in enumerate((left, right)):
+            stage[i, h, :, :HALF], stage[i, h, :, HALF:] = fold(rows)
     loads[2].wait()
     loads[3].wait()
     feats[c, x, :, :whole] = ranges[:, :whole]
@@ -124,14 +133,15 @@
     mark("d_xsend")
     line = ((y, NY, y_peer), (z, NZ, z_peer))
     ring = ((z, NZ, (z_peer(sign), z_peer(-sign))), (y, NY, (y_peer(sign), y_peer(-sign))))
-    for i in range(2):
-        pos, n, peer = line[i]
-        for k in (1, 7, 2, 6, 3, 5, 4):
-            send(stage.at[i], rows8.at[i, pos], sent.at[i], r_w.at[i], peer(k))
+    for h in range(2):
+        for i in range(2):
+            pos, n, peer = line[i]
+            for k in FAR_FIRST:
+                send(stage.at[i, h], rows8.at[i, h, pos], sent.at[i], r_w.at[i, h], peer(k))
     for k in range(1, NX):
         send(feats.at[c, x], feats.at[c, x], sent.at[2], r_f.at[0], x_peer(k))
     for i in range(2):
-        rows8[i, line[i][0]] = stage[i]
+        rows8[i, :, line[i][0]] = stage[i]
     loads[4].wait()
     target_pad[:, :OUTW] = targets[...].astype(F32)
     target_pad[:, whole:] = jnp.concatenate(
@@ -153,20 +163,25 @@
         return step
 
     mark("e_pack")
-    w_steps = []
-    for i in range(2):
-        wait_all(rows8.at[i, 0:7], r_w.at[i])
-        for j in range(8):
-            pack[i, ROWS * j : ROWS * (j + 1)] = rows8[i, j].astype(F32)
-        weights[i, ring[i][0]] = pack[i].astype(BF16)
-        w_steps.append(
-            [
-                ring_gather(lambda o, i=i, p=p: weights.at[i, o, p[0], p[1]], i, lambda j, i=i, q=q: r_ring.at[i, q, j])
-                for q, p in enumerate(W_CHUNKS[i])
-            ]
-        )
-        for step in w_steps[i]:
-            step(0)
+    w_steps = [
+        [
+            ring_gather(lambda o, i=i, p=p: weights.at[i, o, p[0], p[1]], i, lambda j, i=i, q=q: r_ring.at[i, q, j])
+            for q, p in enumerate(W_CHUNKS[i])
+        ]
+        for i in range(2)
+    ]
+    for h in range(2):
+        at = HALF * h
+        for i in range(2):
+            wait_all(rows8.at[i, h, 0:7], r_w.at[i, h])
+            for j in range(8):
+                two = rows8[i, h, j].astype(F32)
+                pack[i, ROWS * j : ROWS * j + 2, at : at + HALF] = two[:, :HALF]
+                pack[i, ROWS * j + 2 : ROWS * j + 3, at : at + SPLIT] = two[0:1, HALF:]
+                pack[i, ROWS * j + 2 : ROWS * j + 3, at + SPLIT : at + HALF] = two[1:2, HALF : 2 * HALF - SPLIT]
+            weights[i, ring[i][0], :, at : at + HALF] = pack[i, :, at : at + HALF].astype(BF16)
+            for step in w_steps[i][3 * h : 3 * h + 3]:
+                step(0)
     mark("f_ring1")
     wait_all(feats.at[0, 0:3], r_f.at[0])
     send(feats.at[c], feats.at[c], sent.at[3], r_f.at[1], partner)
@@ -291,28 +306,39 @@
             for step, last in sums_of[g]:
                 step(k)
     mark("s_xsend")
-    for g in (1, 0):
-        pos, n, peer = line[g]
-        for q, p in enumerate(W_CHUNKS[g]):
-            pack[g, p[0], p[1]] = sums_of[g][q][1]()
-        for j in range(8):
-            line_send[g, j] = pack[g, ROWS * j : ROWS * (j + 1)].astype(BF16)
-        for k in (4, 3, 5, 2, 6, 1, 7):
-            send(line_send.at[g, around(pos, k, n)], line_recv.at[g, pos], sent.at[12 + g], r_line.at[g], peer(k))
-        line_recv[g, pos] = line_send[g, pos]
+    for h in range(2):
+        at = HALF * h
+        for g in (1, 0):
+            pos, n, peer = line[g]
+            for q in range(3 * h, 3 * h + 3):
+                p = W_CHUNKS[g][q]
+                pack[g, p[0], p[1]] = sums_of[g][q][1]()
+            for j in range(8):
+                rows = pack[g, ROWS * j : ROWS * (j + 1), at : at + HALF]
+                line_send[g, h, j, :, :HALF], line_send[g, h, j, :, HALF:] = fold(rows)
+            for k in FAR_FIRST:
+                send(
+                    line_send.at[g, h, around(pos, k, n)], line_recv.at[g, h, pos],
+                    sent.at[12 + g], r_line.at[g, h], peer(k),
+                )
+            line_recv[g, h, pos] = line_send[g, h, pos]
     mark("t_xrecv")
     squares = jnp.zeros((1, 1), F32)
-    for g in (1, 0):
-        to, width = ((grad_in, INW), (grad_out, OUTW))[g]
-        wait_all(line_recv.at[g, 0:7], r_line.at[g])
-        own = line_recv[g, 0].astype(F32)
-        for j in range(1, 8):
-            own = own + line_recv[g, j].astype(F32)
-        own = own[:, :width]
-        to[...] = own
-        stores.append(pltpu.make_async_copy(to, (grad_in_h, grad_out_h)[g], s_in.at[6 + g]))
-        stores[-1].start()
-        squares = squares + jnp.sum(own * own, keepdims=True)
+    for h in range(2):
+        for g in (1, 0):
+            to, width = ((grad_in, INW), (grad_out, OUTW))[g]
+            wait_all(line_recv.at[g, h, 0:7], r_line.at[g, h])
+            own = line_recv[g, h, 0].astype(F32)
+            for j in range(1, 8):
+                own = own + line_recv[g, h, j].astype(F32)
+            at, stop = HALF * h, (HALF, width)[h]
+            to[0:2, at:stop] = own[:, : stop - at]
+            to[2:3, at : at + SPLIT] = own[0:1, HALF:]
+            to[2:3, at + SPLIT : stop] = own[1:2, HALF : HALF + stop - at - SPLIT]
+            if h == 1:
+                stores.append(pltpu.make_async_copy(to, (grad_in_h, grad_out_h)[g], s_in.at[6 + g]))
+                stores[-1].start()
+                squares = squares + jnp.sum(to[...] * to[...], keepdims=True)
 
     mark("u_ar")
     lane = lax.broadcasted_iota(jnp.int32, (1, 128), 1)
@@ -320,7 +346,7 @@
     first = z * 2 + c
     ar_send[0] = total
     ar_zc[first] = total
-    for k in range(1, 16):
+    for k in [1] + [2 * f + i for f in FAR_FIRST for i in range(2)]:
         pz, pc = around(z, k // 2, NZ), (c if k % 2 == 0 else 1 - c)
         send(ar_send.at[0], ar_zc.at[first], sent.at[14], r_ar.at[0], at_dev(x, pz, pc, y))
     wait_all(ar_zc.at[0:15], r_ar.at[0])
@@ -328,23 +354,24 @@
     ar_send[1] = total
     second = x * NY + y
     ar_xy[second] = total
-    for k in range(1, 32):
-        send(
-            ar_send.at[1], ar_xy.at[second], sent.at[15], r_ar.at[1],
-            at_dev(around(x, k // NY, NX), z, c, around(y, k % NY, NY)),
-        )
+    for ky in FAR_FIRST + (0,):
+        for kx in (2, 1, 3, 0):
+            if kx or ky:
+                send(
+                    ar_send.at[1], ar_xy.at[second], sent.at[15], r_ar.at[1],
+                    at_dev(around(x, kx, NX), z, c, around(y, ky, NY)),
+                )
     wait_all(ar_xy.at[0:31], r_ar.at[1])
     total = jnp.sum(ar_xy[...], axis=0)
     sums[...] = total
-    loss[...] = total[:, 1:2] / (BATCH * OUTW)
+    stores.append(pltpu.make_async_copy(sums, sums_h, s_in.at[8]))
+    stores[-1].start()
     mark("w_sends")
-    for store in stores:
-        store.wait()
     for i in range(2):
-        wait_all(rows8.at[i, 0:7], sent.at[i])
+        wait_all(rows8.at[i, :, 0:7], sent.at[i])
         wait_all(weights.at[i, 0:7, :, : (WIDE, WIDE_OUT)[i]], sent.at[4 + i])
         wait_all(ring_send.at[i, :, :, : (WIDE, WIDE_OUT)[i]], sent.at[10 + i])
-        wait_all(line_send.at[i, 0:7], sent.at[12 + i])
+        wait_all(line_send.at[i, :, 0:7], sent.at[12 + i])
     wait_all(feats.at[0, 0:3], sent.at[2])
     wait_all(feats.at[0], sent.at[3])
     wait_all(cross, sent.at[6])
@@ -353,12 +380,14 @@
     wait_all(cross, sent.at[9])
     wait_all(ar_zc.at[0:15], sent.at[14])
     wait_all(ar_xy.at[0:31], sent.at[15])
+    for store in stores:
+        store.wait()
     mark(None)
 
 
 def finish(
-    predicted_i, grad_in_i, grad_out_i, sums_i, predicted_h, update_in_h, update_out_h,
-    predicted, update_in, update_out, sums, r, s,
+    predicted_i, grad_in_i, grad_out_i, sums_i, predicted_h, update_in_h, update_out_h, loss_h,
+    predicted, update_in, update_out, loss, sums, r, s,
 ):
     loads = [
         pltpu.make_async_copy(src, dst, r.at[i])
@@ -369,7 +398,7 @@
     stores = [
         pltpu.make_async_copy(src, dst, s.at[i])
         for i, (src, dst) in enumerate(
-            ((predicted, predicted_h), (update_in, update_in_h), (update_out, update_out_h))
+            ((predicted, predicted_h), (update_in, update_in_h), (update_out, update_out_h), (loss, loss_h))
         )
     ]
     for load in loads:
@@ -377,6 +406,8 @@
     loads[1].wait()
     stores[0].start()
     loads[0].wait()
+    loss[...] = sums[:, 1:2] / (BATCH * OUTW)
+    stores[3].start()
     scale = lax.rsqrt(sums[:, 0:1] / (HIDDEN * (INW + OUTW)) + 1e-6)
     for i, update in ((1, update_in), (2, update_out)):
         loads[i + 1].wait()
@@ -387,20 +418,20 @@
 
 
 def body(ranges, board, targets, w_in, w_out):
-    vmem = pl.BlockSpec(memory_space=pltpu.VMEM)
     hbm = pl.BlockSpec(memory_space=pltpu.HBM)
     dma = pltpu.SemaphoreType.DMA
     scratch = [
         pltpu.VMEM((STATES, OUTW), BF16),
         pltpu.VMEM((ROWS, INW), F32),
         pltpu.VMEM((ROWS, OUTW), F32),
+        pltpu.VMEM((1, 128), F32),
         pltpu.VMEM((STATES, OUTW), BF16),
         pltpu.VMEM((5, STATES), jnp.int32),
         pltpu.VMEM((STATES, OUTW), BF16),
         pltpu.VMEM((ROWS, INW), BF16),
         pltpu.VMEM((ROWS, OUTW), BF16),
-        pltpu.VMEM((2, ROWS, WIDE), BF16),
-        pltpu.VMEM((2, 8, ROWS, WIDE), BF16),
+        pltpu.VMEM((2, 2, 2, PACKED), BF16),
+        pltpu.VMEM((2, 2, 8, 2, PACKED), BF16),
         pltpu.VMEM((2, LINE, WIDE), F32),
         pltpu.VMEM((2, 8, LINE, WIDE), BF16),
         pltpu.VMEM((2, NX, STATES, WIDE), BF16),
@@ -418,29 +449,28 @@
         pltpu.VMEM((2, 7, LINE, WIDE), BF16),
         pltpu.VMEM((2, LONG, LINE, WIDE), BF16),
         pltpu.VMEM((2, SHORT, LINE, WIDE), BF16),
-        pltpu.VMEM((2, 8, ROWS, WIDE), BF16),
-        pltpu.VMEM((2, 8, ROWS, WIDE), BF16),
+        pltpu.VMEM((2, 2, 8, 2, PACKED), BF16),
+        pltpu.VMEM((2, 2, 8, 2, PACKED), BF16),
         pltpu.VMEM((2, 1, 128), F32),
         pltpu.VMEM((16, 1, 128), F32),
         pltpu.VMEM((32, 1, 128), F32),
-        dma((8,)),
+        dma((9,)),
         dma((16,)),
     ]
-    for shape in ((2,), (2, 6, 7), (2,), (5,), (4,), (4,), (2,), (2,)):
+    for shape in ((2, 2), (2, 6, 7), (2,), (5,), (4,), (4,), (2, 2), (2,)):
         scratch.append(dma(shape))
     made = (
         jax.ShapeDtypeStruct((STATES, OUTW), BF16),
         jax.ShapeDtypeStruct((ROWS, INW), F32),
         jax.ShapeDtypeStruct((ROWS, OUTW), F32),
         jax.ShapeDtypeStruct((1, 128), F32),
-        jax.ShapeDtypeStruct((1, 1), F32),
     )
     made = pl.pallas_call(
         kernel,
         name="step",
         out_shape=made,
         in_specs=[hbm] * 5,
-        out_specs=(hbm, hbm, hbm, vmem, vmem),
+        out_specs=(hbm,) * 4,
         scratch_shapes=scratch,
         compiler_params=pltpu.CompilerParams(
             collective_id=0, has_side_effects=True, vmem_limit_bytes=VMEM_STEP
@@ -450,24 +480,26 @@
         jax.ShapeDtypeStruct((STATES, OUTW), BF16),
         jax.ShapeDtypeStruct((ROWS, INW), F32),
         jax.ShapeDtypeStruct((ROWS, OUTW), F32),
+        jax.ShapeDtypeStruct((1, 1), F32),
     )
     outs = pl.pallas_call(
         finish,
         name="finish",
         out_shape=outs,
         in_specs=[hbm] * 4,
-        out_specs=(hbm,) * 3,
+        out_specs=(hbm,) * 4,
         scratch_shapes=[
             pltpu.VMEM((STATES, OUTW), BF16),
             pltpu.VMEM((ROWS, INW), F32),
             pltpu.VMEM((ROWS, OUTW), F32),
+            pltpu.VMEM((1, 1), F32),
             pltpu.VMEM((1, 128), F32),
             dma((4,)),
-            dma((3,)),
+            dma((4,)),
         ],
         compiler_params=pltpu.CompilerParams(vmem_limit_bytes=VMEM_STEP),
-    )(*made[:4])
-    return outs[0], outs[1], outs[2], made[4][0, 0]
+    )(*made)
+    return outs[0], outs[1], outs[2], outs[3][0, 0]
 
 
 def solution(mesh):

time: 93.3 us -> 87.1 us (0.934)
  Pallas kernels: 90.7 us -> 86.2 us
  between operations: 2.4 us -> 0.64 us
    pallas_call x1, Pallas kernels: 89 us -> 84.5 us  [body(): pl.pallas_call(kernel, name='step', out_shape=made, in_specs=[hbm] * 5, o...]
where the time goes in v4:
time: 87.1 us; the launch traced here: 86.9 us
  Pallas kernels  86.2 us (99%)
    pallas_call x1, Pallas kernels, body(): pl.pallas_call(kernel, name='step', out_shape=made, in_specs=[hbm] * 5, o...  84.5 us
    pallas_call x1, Pallas kernels, body(): pl.pallas_call(finish, name='finish', out_shape=outs, in_specs=[hbm] * 4,...  1.74 us

profile of v4, /device:TPU:1, one launch (start us, length us, event | category | flops | bytes accessed | tf_op | source)
XLA Modules:
  0.0 86.9 jit_solution(4790789430005778265)
XLA Ops:
  0.6 84.5 %step.1 = (bf16[16,2652]{1,0:T(8,128)(2,1)}, f32[3,2704]{1,0:T(4,128)}, f32[3,2652]{1,0:T(4,128)}, f32[1,128]{1,0:T(1,128)}) custom-call(bf16[16,2652]{1,0:T(8,128)(2,1)} %ranges_h.1, s32[5,16]{1,0:T(8,128)} %bitcast.2, bf16[16,2652]{1,0:T(8,128)(2,1)} %targets_h.1, bf16[3,2704]{1,0:T(4,128)(2,1)} %w_in_h.1, bf16[3,2652]{1,0:T(4,128)(2,1)} %w_out_h.1), custom_call_target="tpu_custom_call" | custom-call | tf_op jit(solution)/shard_map/step/pallas_call | solution.py:468
  85.1 1.7 %finish.1 = (bf16[16,2652]{1,0:T(8,128)(2,1)}, f32[3,2704]{1,0:T(4,128)}, f32[3,2652]{1,0:T(4,128)}, f32[1,1]{1,0:T(1,128)}) custom-call(bf16[16,2652]{1,0:T(8,128)(2,1)} %get-tuple-element.12.predicted_i, f32[3,2704]{1,0:T(4,128)} %get-tuple-element.13.grad_in_i, f32[3,2652]{1,0:T(4,128)} %get-tuple-element.14.grad_out_i, f32[1,128]{1,0:T(1,128)} %get-tuple-element.15.sums_i), custom_call_target="tpu_custom_call" | custom-call | tf_op jit(solution)/shard_map/finish/pallas_call | solution.py:485

commit v5 on v4

--- a/solution.py
+++ b/solution.py
@@ -12,21 +12,33 @@
 NX, NZ, NY = 4, 8, 8
 ROWS, LINE, STATES = 3, 24, 16
 INW, OUTW, HIDDEN, BATCH = 2704, 2652, 1536, 8192
-WIDE, WIDE_OUT, HALF = 2816, 2688, 1408
-SPLIT, PACKED = 768, 2176
-LONG, SHORT = 4, 3
+WIDE, WIDE_OUT = 2816, 2688
+STEPS = 3
 FAR_FIRST = (4, 3, 5, 2, 6, 1, 7)
 GELU_A, GELU_B = 0.7978845608028654, 0.044715
+ALL = slice(0, WIDE)
 O_CHUNKS = tuple(slice(128 * a, 128 * b) for a, b in ((0, 6), (6, 11), (11, 16), (16, 21)))
+PIECES = tuple(slice(128 * a, 128 * b) for a, b in ((0, 6), (6, 14), (14, 22)))
 W_CHUNKS = tuple(
-    tuple((slice(8 * i, 8 * i + 8), slice(a, b)) for a, b in ((0, HALF), (HALF, width)) for i in range(3))
-    for width in (WIDE, WIDE_OUT)
+    tuple(slice(128 * a, 128 * b) for a, b in ((0, 3), (3, 6), (6, 10), (10, 14), (14, 18), (18, last)))
+    for last in (22, 21)
 )
+PLACES = tuple(slice(p.start * 3 // 2, p.stop * 3 // 2) for p in PIECES)
+PACKED = WIDE * 3 // 2
 
 
 def fold(rows):
-    third = jnp.concatenate([rows[2:3, SPLIT:], jnp.zeros((1, PACKED - 2 * HALF + SPLIT), F32)], axis=1)
-    return rows[0:2].astype(BF16), jnp.concatenate([rows[2:3, :SPLIT], third], axis=0).astype(BF16)
+    half = rows.shape[1] // 2
+    third = jnp.concatenate([rows[2:3, :half], rows[2:3, half:]], axis=0)
+    return jnp.concatenate([rows[0:2], third], axis=1).astype(BF16)
+
+
+def unfold(two, put):
+    width = two.shape[1] * 2 // 3
+    half = width // 2
+    put(slice(0, 2), 0, two[:, :width])
+    put(slice(2, 3), 0, two[0:1, width:])
+    put(slice(2, 3), half, two[1:2, width:])
 
 
 def nt(a, b):
@@ -42,7 +54,7 @@
     predicted_h, grad_in_h, grad_out_h, sums_h,
     predicted, grad_in, grad_out, sums, ranges, board, targets, w_in, w_out,
     stage, rows8, pack, weights, feats, values_grad, hidden_t, partial, cross, crossed, to_x, from_x,
-    target_pad, hold, order, mine, ring_send, ring_long, ring_short, line_send, line_recv,
+    target_pad, hold, order, mine, ring_send, ring_came, line_send, line_recv,
     ar_send, ar_zc, ar_xy, s_in, sent,
     r_w, r_ring, r_f, r_cross, r_sum, r_grad, r_line, r_ar,
 ):
@@ -109,10 +121,9 @@
     whole = OUTW // 128 * 128
     for i, (w, width) in enumerate(((w_in, INW), (w_out, OUTW))):
         loads[i].wait()
-        left = w[:, :HALF].astype(F32)
-        right = jnp.concatenate([w[:, HALF:].astype(F32), jnp.zeros((ROWS, WIDE - width), F32)], axis=1)
-        for h, rows in enumerate((left, right)):
-            stage[i, h, :, :HALF], stage[i, h, :, HALF:] = fold(rows)
+        rows = jnp.concatenate([w[...].astype(F32), jnp.zeros((ROWS, WIDE - width), F32)], axis=1)
+        for p, place in zip(PIECES, PLACES):
+            stage[i, :, place] = fold(rows[:, p])
     loads[2].wait()
     loads[3].wait()
     feats[c, x, :, :whole] = ranges[:, :whole]
@@ -132,16 +143,18 @@
 
     mark("d_xsend")
     line = ((y, NY, y_peer), (z, NZ, z_peer))
-    ring = ((z, NZ, (z_peer(sign), z_peer(-sign))), (y, NY, (y_peer(sign), y_peer(-sign))))
-    for h in range(2):
+    ring = tuple(
+        (pos, n, (peer(sign), peer(-sign), peer(2 * sign))) for pos, n, peer in ((z, NZ, z_peer), (y, NY, y_peer))
+    )
+    for h, place in enumerate(PLACES):
         for i in range(2):
             pos, n, peer = line[i]
             for k in FAR_FIRST:
-                send(stage.at[i, h], rows8.at[i, h, pos], sent.at[i], r_w.at[i, h], peer(k))
+                send(stage.at[i, :, place], rows8.at[i, pos, :, place], sent.at[i], r_w.at[i, h], peer(k))
     for k in range(1, NX):
         send(feats.at[c, x], feats.at[c, x], sent.at[2], r_f.at[0], x_peer(k))
     for i in range(2):
-        rows8[i, :, line[i][0]] = stage[i]
+        rows8[i, line[i][0]] = stage[i]
     loads[4].wait()
     target_pad[:, :OUTW] = targets[...].astype(F32)
     target_pad[:, whole:] = jnp.concatenate(
@@ -153,52 +166,59 @@
         copies = {}
 
         def step(k):
-            for way, steps in ((0, LONG), (1, SHORT)):
-                if k >= 1 and k - 1 < steps:
-                    copies[way, k - 1].wait_recv()
-                if k < steps:
-                    block = block_of(around(pos, -k * sign if way == 0 else k * sign, n))
-                    copies[way, k] = send(block, block, sent.at[4 + i], r(way * LONG + k), to[way])
+            if k >= 1:
+                copies[k - 1].wait_recv()
+            if k < STEPS:
+                block = block_of(around(pos, -k * sign, n))
+                if k == STEPS - 1:
+                    copies[3] = send(block, block, sent.at[4 + i], r(3), to[2])
+                copies[k] = send(block, block, sent.at[4 + i], r(k), to[0])
+            if k >= 1:
+                copies[3 + k].wait_recv()
+            if k < STEPS:
+                block = block_of(around(pos, k * sign, n))
+                copies[4 + k] = send(block, block, sent.at[4 + i], r(4 + k), to[1])
+            else:
+                copies[3].wait_recv()
 
         return step
 
     mark("e_pack")
     w_steps = [
         [
-            ring_gather(lambda o, i=i, p=p: weights.at[i, o, p[0], p[1]], i, lambda j, i=i, q=q: r_ring.at[i, q, j])
+            ring_gather(lambda o, i=i, p=p: weights.at[i, o, :, p], i, lambda j, i=i, q=q: r_ring.at[i, q, j])
             for q, p in enumerate(W_CHUNKS[i])
         ]
         for i in range(2)
     ]
-    for h in range(2):
-        at = HALF * h
+    for h, (piece, place) in enumerate(zip(PIECES, PLACES)):
         for i in range(2):
-            wait_all(rows8.at[i, h, 0:7], r_w.at[i, h])
+            wait_all(rows8.at[i, 0:7, :, place], r_w.at[i, h])
             for j in range(8):
-                two = rows8[i, h, j].astype(F32)
-                pack[i, ROWS * j : ROWS * j + 2, at : at + HALF] = two[:, :HALF]
-                pack[i, ROWS * j + 2 : ROWS * j + 3, at : at + SPLIT] = two[0:1, HALF:]
-                pack[i, ROWS * j + 2 : ROWS * j + 3, at + SPLIT : at + HALF] = two[1:2, HALF : 2 * HALF - SPLIT]
-            weights[i, ring[i][0], :, at : at + HALF] = pack[i, :, at : at + HALF].astype(BF16)
-            for step in w_steps[i][3 * h : 3 * h + 3]:
+
+                def put(rows, at, value, i=i, j=j, piece=piece):
+                    at = piece.start + at
+                    pack[i, ROWS * j + rows.start : ROWS * j + rows.stop, at : at + value.shape[1]] = value
+
+                unfold(rows8[i, j, :, place].astype(F32), put)
+            weights[i, ring[i][0], :, piece] = pack[i, :, piece].astype(BF16)
+            for step in w_steps[i][2 * h : 2 * h + 2]:
                 step(0)
     mark("f_ring1")
     wait_all(feats.at[0, 0:3], r_f.at[0])
     send(feats.at[c], feats.at[c], sent.at[3], r_f.at[1], partner)
-    for k in range(1, LONG + 1):
+    for k in range(1, STEPS + 1):
         for steps in zip(*w_steps):
             for step in steps:
                 step(k)
     mark("g_across")
     wait_all(feats.at[1 - c], r_f.at[1])
 
-    def units(i):
-        if i == 0:
-            return weights[0].reshape(NZ * LINE, WIDE)
-        return weights[1, :, :, :WIDE_OUT].reshape(NY * LINE, WIDE_OUT)
-
-    def states(ref, width):
-        return ref[:, :, :, :width].reshape(2 * NX * STATES, width)
+    def units(i, p):
+        return weights[i, :, :, p].reshape(8 * LINE, p.stop - p.start)
+
+    def states(ref, p):
+        return ref[:, :, :, p].reshape(2 * NX * STATES, p.stop - p.start)
 
     def reorder(src, dst):
         for a in range(8):
@@ -206,7 +226,7 @@
                 dst[b, ROWS * a : ROWS * (a + 1)] = src[a, ROWS * b : ROWS * (b + 1)]
 
     mark("h_pre")
-    order[0] = nt(units(0), states(feats, WIDE)).reshape(NZ, LINE, 2 * NX * STATES)
+    order[0] = nt(units(0, ALL), states(feats, ALL)).reshape(NZ, LINE, 2 * NX * STATES)
     reorder(order.at[0], order.at[1])
     pre = order[1].reshape(NY * LINE, 2 * NX * STATES)
     tanh = jnp.tanh(GELU_A * (pre + GELU_B * pre * pre * pre))
@@ -217,12 +237,12 @@
     hidden_t[...] = hidden.T.astype(BF16).reshape(2, NX * STATES, NY * LINE)
 
     mark("i_partial")
-    cross[...] = nn(hidden_t[1 - c], units(1)).astype(BF16).reshape(NX, STATES, WIDE_OUT)
     for q, p in enumerate(O_CHUNKS):
+        cross[:, :, p] = nn(hidden_t[1 - c], units(1, p)).astype(BF16).reshape(NX, STATES, p.stop - p.start)
         send(cross.at[:, :, p], crossed.at[:, :, p], sent.at[6], r_cross.at[q], partner)
-    partial[...] = nn(hidden_t[c], units(1)).reshape(NX, STATES, WIDE_OUT)
     mark("j_rs")
     for q, p in enumerate(O_CHUNKS):
+        partial[:, :, p] = nn(hidden_t[c], units(1, p)).reshape(NX, STATES, p.stop - p.start)
         wait_all(crossed.at[:, :, p], r_cross.at[q])
         for k in (2, 1, 3):
             px = around(x, k, NX)
@@ -247,95 +267,107 @@
         predicted[:, p.start : right] = summed[:, : right - p.start].astype(BF16)
     stores = [pltpu.make_async_copy(predicted, predicted_h, s_in.at[5])]
     stores[0].start()
+    def ring_sum(g, q, p):
+        pos, n, to = ring[g]
+        copies = {}
+
+        def term(move):
+            return mine[g, around(pos, move, n), :, p]
+
+        def came(j):
+            copies[j].wait_recv()
+            return ring_came[g, j, :, p].astype(F32)
+
+        def pass_on(j, value, way):
+            out = ring_send.at[g, j, :, p]
+            out[...] = value.astype(BF16)
+            sem = r_ring.at[g, q, 7 if j == 3 else j]
+            copies[j] = send(out, ring_came.at[g, j, :, p], sent.at[10 + g], sem, to[way])
+
+        def step(k):
+            if k == 0:
+                pass_on(3, term(4 * sign), 2)
+                pass_on(0, term(3 * sign), 0)
+                pass_on(4, term(-3 * sign), 1)
+            else:
+                value = term((STEPS - k) * sign) + came(k - 1)
+                pass_on(k, value + came(3) if k == 1 else value, 0)
+                pass_on(4 + k, term(-(STEPS - k) * sign) + came(3 + k), 1)
+
+        def last():
+            return term(0) + came(6) + came(2)
+
+        return step, last
+
+    sums_of = {g: [ring_sum(g, q, p) for q, p in enumerate(W_CHUNKS[g])] for g in (1, 0)}
+    hidden_b = hold[0].astype(BF16)
+
+    def backward(q, total):
+        p = O_CHUNKS[q]
+        wait_all(values_grad.at[1 - c, :, :, p], r_cross.at[4 + q])
+        grad = states(values_grad, p)
+        mine[1, :, :, p] = nn(hidden_b, grad).reshape(NY, LINE, p.stop - p.start)
+        for step, last in sums_of[1][(0, 2, 2, 4)[q] : (2, 2, 4, 6)[q]]:
+            step(0)
+        more = nt(units(1, p), grad)
+        return more if total is None else total + more
+
     mark("l_ag")
+    hidden_grad = None
     for q, p in enumerate(O_CHUNKS):
         wait_all(from_x.at[0:3, :, p], r_grad.at[q])
         block = values_grad.at[c, :, :, p]
-        send(block, block, sent.at[9], r_cross.at[4], partner)
-    wait_all(values_grad.at[1 - c, :, :, :WIDE_OUT], r_cross.at[4])
-
-    def ring_sum(g, q, p):
-        pos, n, to = ring[g]
-        copies = {}
-
-        def came(way, k):
-            return (ring_long, ring_short)[way].at[g, k, p[0], p[1]]
-
-        def term(t):
-            return mine[g, t, p[0], p[1]]
-
-        def step(k):
-            for way, steps in ((0, LONG), (1, SHORT)):
-                if k < steps:
-                    move = (steps - k) * sign if way == 0 else -(steps - k) * sign
-                    value = term(around(pos, move, n))
-                    if k >= 1:
-                        copies[way, k - 1].wait_recv()
-                        value = value + came(way, k - 1)[...].astype(F32)
-                    j = way * LONG + k
-                    out = ring_send.at[g, j, p[0], p[1]]
-                    out[...] = value.astype(BF16)
-                    copies[way, k] = send(out, came(way, k), sent.at[10 + g], r_ring.at[g, q, j], to[way])
-
-        def last():
-            value = term(pos)
-            for way, steps in ((1, SHORT), (0, LONG)):
-                copies[way, steps - 1].wait_recv()
-                value = value + came(way, steps - 1)[...].astype(F32)
-            return value
-
-        return step, last
-
+        send(block, block, sent.at[9], r_cross.at[4 + q], partner)
+        if q:
+            hidden_grad = backward(q - 1, hidden_grad)
     mark("m_gout")
-    sums_of = {g: [ring_sum(g, q, p) for q, p in enumerate(W_CHUNKS[g])] for g in (1, 0)}
-    mine[1, :, :, :WIDE_OUT] = nn(hold[0].astype(BF16), states(values_grad, WIDE_OUT)).reshape(NY, LINE, WIDE_OUT)
-    for step, last in sums_of[1]:
-        step(0)
+    hidden_grad = backward(3, hidden_grad)
     mark("n_hgrad")
-    hidden_grad = nt(units(1), states(values_grad, WIDE_OUT))
     order[1] = (hidden_grad * hold[1]).reshape(NY, LINE, 2 * NX * STATES)
     reorder(order.at[1], order.at[0])
     pre_grad = order[0].reshape(NZ * LINE, 2 * NX * STATES).astype(BF16)
     mark("p_gin")
-    mine[0] = nn(pre_grad, states(feats, WIDE)).reshape(NZ, LINE, WIDE)
-    for step, last in sums_of[0]:
-        step(0)
+    for h, piece in enumerate(PIECES):
+        mine[0, :, :, piece] = nn(pre_grad, states(feats, piece)).reshape(NZ, LINE, piece.stop - piece.start)
+        for step, last in sums_of[0][2 * h : 2 * h + 2]:
+            step(0)
     mark("r_zring")
-    for k in range(1, LONG):
+    for k in range(1, STEPS):
         for g in (1, 0):
             for step, last in sums_of[g]:
                 step(k)
     mark("s_xsend")
-    for h in range(2):
-        at = HALF * h
+    for h, (piece, place) in enumerate(zip(PIECES, PLACES)):
         for g in (1, 0):
             pos, n, peer = line[g]
-            for q in range(3 * h, 3 * h + 3):
+            for q in range(2 * h, 2 * h + 2):
                 p = W_CHUNKS[g][q]
-                pack[g, p[0], p[1]] = sums_of[g][q][1]()
+                pack[g, :, p] = sums_of[g][q][1]()
             for j in range(8):
-                rows = pack[g, ROWS * j : ROWS * (j + 1), at : at + HALF]
-                line_send[g, h, j, :, :HALF], line_send[g, h, j, :, HALF:] = fold(rows)
+                line_send[g, j, :, place] = fold(pack[g, ROWS * j : ROWS * (j + 1), piece])
             for k in FAR_FIRST:
                 send(
-                    line_send.at[g, h, around(pos, k, n)], line_recv.at[g, h, pos],
+                    line_send.at[g, around(pos, k, n), :, place], line_recv.at[g, pos, :, place],
                     sent.at[12 + g], r_line.at[g, h], peer(k),
                 )
-            line_recv[g, h, pos] = line_send[g, h, pos]
+            line_recv[g, pos, :, place] = line_send[g, pos, :, place]
     mark("t_xrecv")
     squares = jnp.zeros((1, 1), F32)
-    for h in range(2):
+    for h, (piece, place) in enumerate(zip(PIECES, PLACES)):
         for g in (1, 0):
             to, width = ((grad_in, INW), (grad_out, OUTW))[g]
-            wait_all(line_recv.at[g, h, 0:7], r_line.at[g, h])
-            own = line_recv[g, h, 0].astype(F32)
+            wait_all(line_recv.at[g, 0:7, :, place], r_line.at[g, h])
+            own = line_recv[g, 0, :, place].astype(F32)
             for j in range(1, 8):
-                own = own + line_recv[g, h, j].astype(F32)
-            at, stop = HALF * h, (HALF, width)[h]
-            to[0:2, at:stop] = own[:, : stop - at]
-            to[2:3, at : at + SPLIT] = own[0:1, HALF:]
-            to[2:3, at + SPLIT : stop] = own[1:2, HALF : HALF + stop - at - SPLIT]
-            if h == 1:
+                own = own + line_recv[g, j, :, place].astype(F32)
+
+            def put(rows, at, value, to=to, width=width, piece=piece):
+                at = piece.start + at
+                stop = min(at + value.shape[1], width)
+                to[rows, at:stop] = value[:, : stop - at]
+
+            unfold(own, put)
+            if h == len(PIECES) - 1:
                 stores.append(pltpu.make_async_copy(to, (grad_in_h, grad_out_h)[g], s_in.at[6 + g]))
                 stores[-1].start()
                 squares = squares + jnp.sum(to[...] * to[...], keepdims=True)
@@ -368,10 +400,10 @@
     stores[-1].start()
     mark("w_sends")
     for i in range(2):
-        wait_all(rows8.at[i, :, 0:7], sent.at[i])
+        wait_all(rows8.at[i, 0:7], sent.at[i])
         wait_all(weights.at[i, 0:7, :, : (WIDE, WIDE_OUT)[i]], sent.at[4 + i])
         wait_all(ring_send.at[i, :, :, : (WIDE, WIDE_OUT)[i]], sent.at[10 + i])
-        wait_all(line_send.at[i, :, 0:7], sent.at[12 + i])
+        wait_all(line_send.at[i, 0:7], sent.at[12 + i])
     wait_all(feats.at[0, 0:3], sent.at[2])
     wait_all(feats.at[0], sent.at[3])
     wait_all(cross, sent.at[6])
@@ -430,8 +462,8 @@
         pltpu.VMEM((STATES, OUTW), BF16),
         pltpu.VMEM((ROWS, INW), BF16),
         pltpu.VMEM((ROWS, OUTW), BF16),
-        pltpu.VMEM((2, 2, 2, PACKED), BF16),
-        pltpu.VMEM((2, 2, 8, 2, PACKED), BF16),
+        pltpu.VMEM((2, 2, PACKED), BF16),
+        pltpu.VMEM((2, 8, 2, PACKED), BF16),
         pltpu.VMEM((2, LINE, WIDE), F32),
         pltpu.VMEM((2, 8, LINE, WIDE), BF16),
         pltpu.VMEM((2, NX, STATES, WIDE), BF16),
@@ -447,17 +479,16 @@
         pltpu.VMEM((2, 8, LINE, 2 * NX * STATES), F32),
         pltpu.VMEM((2, 8, LINE, WIDE), F32),
         pltpu.VMEM((2, 7, LINE, WIDE), BF16),
-        pltpu.VMEM((2, LONG, LINE, WIDE), BF16),
-        pltpu.VMEM((2, SHORT, LINE, WIDE), BF16),
-        pltpu.VMEM((2, 2, 8, 2, PACKED), BF16),
-        pltpu.VMEM((2, 2, 8, 2, PACKED), BF16),
+        pltpu.VMEM((2, 7, LINE, WIDE), BF16),
+        pltpu.VMEM((2, 8, 2, PACKED), BF16),
+        pltpu.VMEM((2, 8, 2, PACKED), BF16),
         pltpu.VMEM((2, 1, 128), F32),
         pltpu.VMEM((16, 1, 128), F32),
         pltpu.VMEM((32, 1, 128), F32),
         dma((9,)),
         dma((16,)),
     ]
-    for shape in ((2, 2), (2, 6, 7), (2,), (5,), (4,), (4,), (2, 2), (2,)):
+    for shape in ((2, 3), (2, 6, 8), (2,), (8,), (4,), (4,), (2, 3), (2,)):
         scratch.append(dma(shape))
     made = (
         jax.ShapeDtypeStruct((STATES, OUTW), BF16),

time: 87.1 us -> 82.7 us (0.949)
  Pallas kernels: 86.2 us -> 81.9 us
    pallas_call x1, Pallas kernels: 84.5 us -> 80.2 us  [body(): pl.pallas_call(kernel, name='step', out_shape=made, in_specs=[hbm] * 5, o...]
where the time goes in v5:
time: 82.7 us; the launch traced here: 82.6 us
  Pallas kernels  81.9 us (99%)
    pallas_call x1, Pallas kernels, body(): pl.pallas_call(kernel, name='step', out_shape=made, in_specs=[hbm] * 5, o...  80.2 us
    pallas_call x1, Pallas kernels, body(): pl.pallas_call(finish, name='finish', out_shape=outs, in_specs=[hbm] * 4,...  1.74 us

profile of v5, /device:TPU:1, one launch (start us, length us, event | category | flops | bytes accessed | tf_op | source)
XLA Modules:
  0.0 82.6 jit_solution(14616097145618265835)
XLA Ops:
  0.6 80.2 %step.1 = (bf16[16,2652]{1,0:T(8,128)(2,1)}, f32[3,2704]{1,0:T(4,128)}, f32[3,2652]{1,0:T(4,128)}, f32[1,128]{1,0:T(1,128)}) custom-call(bf16[16,2652]{1,0:T(8,128)(2,1)} %ranges_h.1, s32[5,16]{1,0:T(8,128)} %bitcast.2, bf16[16,2652]{1,0:T(8,128)(2,1)} %targets_h.1, bf16[3,2704]{1,0:T(4,128)(2,1)} %w_in_h.1, bf16[3,2652]{1,0:T(4,128)(2,1)} %w_out_h.1), custom_call_target="tpu_custom_call" | custom-call | tf_op jit(solution)/shard_map/step/pallas_call | solution.py:499
  80.8 1.7 %finish.1 = (bf16[16,2652]{1,0:T(8,128)(2,1)}, f32[3,2704]{1,0:T(4,128)}, f32[3,2652]{1,0:T(4,128)}, f32[1,1]{1,0:T(1,128)}) custom-call(bf16[16,2652]{1,0:T(8,128)(2,1)} %get-tuple-element.12.predicted_i, f32[3,2704]{1,0:T(4,128)} %get-tuple-element.13.grad_in_i, f32[3,2652]{1,0:T(4,128)} %get-tuple-element.14.grad_out_i, f32[1,128]{1,0:T(1,128)} %get-tuple-element.15.sums_i), custom_call_target="tpu_custom_call" | custom-call | tf_op jit(solution)/shard_map/finish/pallas_call | solution.py:516

commit v6 on v5

--- a/solution.py
+++ b/solution.py
@@ -16,14 +16,16 @@
 STEPS = 3
 FAR_FIRST = (4, 3, 5, 2, 6, 1, 7)
 GELU_A, GELU_B = 0.7978845608028654, 0.044715
-ALL = slice(0, WIDE)
-O_CHUNKS = tuple(slice(128 * a, 128 * b) for a, b in ((0, 6), (6, 11), (11, 16), (16, 21)))
-PIECES = tuple(slice(128 * a, 128 * b) for a, b in ((0, 6), (6, 14), (14, 22)))
-W_CHUNKS = tuple(
-    tuple(slice(128 * a, 128 * b) for a, b in ((0, 3), (3, 6), (6, 10), (10, 14), (14, 18), (18, last)))
-    for last in (22, 21)
-)
-PLACES = tuple(slice(p.start * 3 // 2, p.stop * 3 // 2) for p in PIECES)
+def columns(*cuts):
+    return tuple(slice(128 * a, 128 * b) for a, b in zip(cuts, cuts[1:]))
+
+
+PIECES = (columns(0, 4, 8, 12, 16, 20, 22), columns(0, 4, 8, 10, 14, 18, 22))
+W_CHUNKS = (PIECES[0], columns(0, 4, 8, 10, 14, 18, 21))
+O_CHUNKS = W_CHUNKS[1]
+AXIS = (0, 0, 0, 1, 1, 1)
+ORDER = (0, 3, 1, 4, 2, 5)
+PLACES = tuple(tuple(slice(p.start * 3 // 2, p.stop * 3 // 2) for p in pieces) for pieces in PIECES)
 PACKED = WIDE * 3 // 2
 
 
@@ -122,7 +124,7 @@
     for i, (w, width) in enumerate(((w_in, INW), (w_out, OUTW))):
         loads[i].wait()
         rows = jnp.concatenate([w[...].astype(F32), jnp.zeros((ROWS, WIDE - width), F32)], axis=1)
-        for p, place in zip(PIECES, PLACES):
+        for p, place in zip(PIECES[i], PLACES[i]):
             stage[i, :, place] = fold(rows[:, p])
     loads[2].wait()
     loads[3].wait()
@@ -146,23 +148,25 @@
     ring = tuple(
         (pos, n, (peer(sign), peer(-sign), peer(2 * sign))) for pos, n, peer in ((z, NZ, z_peer), (y, NY, y_peer))
     )
-    for h, place in enumerate(PLACES):
-        for i in range(2):
-            pos, n, peer = line[i]
+    for i in range(2):
+        for q in ORDER:
+            pos, n, peer = line[AXIS[q]]
+            place = PLACES[i][q]
             for k in FAR_FIRST:
-                send(stage.at[i, :, place], rows8.at[i, pos, :, place], sent.at[i], r_w.at[i, h], peer(k))
+                send(stage.at[i, :, place], rows8.at[i, pos, :, place], sent.at[i], r_w.at[i, q], peer(k))
     for k in range(1, NX):
         send(feats.at[c, x], feats.at[c, x], sent.at[2], r_f.at[0], x_peer(k))
     for i in range(2):
-        rows8[i, line[i][0]] = stage[i]
+        for axis, place in zip(AXIS, PLACES[i]):
+            rows8[i, line[axis][0], :, place] = stage[i, :, place]
     loads[4].wait()
     target_pad[:, :OUTW] = targets[...].astype(F32)
     target_pad[:, whole:] = jnp.concatenate(
         [targets[:, whole:].astype(F32), jnp.zeros((STATES, WIDE_OUT - OUTW), F32)], axis=1
     )
 
-    def ring_gather(block_of, i, r):
-        pos, n, to = ring[i]
+    def ring_gather(block_of, i, axis, r):
+        pos, n, to = ring[axis]
         copies = {}
 
         def step(k):
@@ -186,14 +190,15 @@
     mark("e_pack")
     w_steps = [
         [
-            ring_gather(lambda o, i=i, p=p: weights.at[i, o, :, p], i, lambda j, i=i, q=q: r_ring.at[i, q, j])
+            ring_gather(lambda o, i=i, p=p: weights.at[i, o, :, p], i, AXIS[q], lambda j, i=i, q=q: r_ring.at[i, q, j])
             for q, p in enumerate(W_CHUNKS[i])
         ]
         for i in range(2)
     ]
-    for h, (piece, place) in enumerate(zip(PIECES, PLACES)):
-        for i in range(2):
-            wait_all(rows8.at[i, 0:7, :, place], r_w.at[i, h])
+    for i in range(2):
+        for q in ORDER:
+            piece, place = PIECES[i][q], PLACES[i][q]
+            wait_all(rows8.at[i, 0:7, :, place], r_w.at[i, q])
             for j in range(8):
 
                 def put(rows, at, value, i=i, j=j, piece=piece):
@@ -201,17 +206,15 @@
                     pack[i, ROWS * j + rows.start : ROWS * j + rows.stop, at : at + value.shape[1]] = value
 
                 unfold(rows8[i, j, :, place].astype(F32), put)
-            weights[i, ring[i][0], :, piece] = pack[i, :, piece].astype(BF16)
-            for step in w_steps[i][2 * h : 2 * h + 2]:
-                step(0)
+            weights[i, ring[AXIS[q]][0], :, piece] = pack[i, :, piece].astype(BF16)
+            w_steps[i][q](0)
     mark("f_ring1")
     wait_all(feats.at[0, 0:3], r_f.at[0])
     send(feats.at[c], feats.at[c], sent.at[3], r_f.at[1], partner)
-    for k in range(1, STEPS + 1):
-        for steps in zip(*w_steps):
-            for step in steps:
-                step(k)
-    mark("g_across")
+    for k in range(1, STEPS):
+        for i in range(2):
+            for q in ORDER:
+                w_steps[i][q](k)
     wait_all(feats.at[1 - c], r_f.at[1])
 
     def units(i, p):
@@ -226,31 +229,54 @@
                 dst[b, ROWS * a : ROWS * (a + 1)] = src[a, ROWS * b : ROWS * (b + 1)]
 
     mark("h_pre")
-    order[0] = nt(units(0, ALL), states(feats, ALL)).reshape(NZ, LINE, 2 * NX * STATES)
-    reorder(order.at[0], order.at[1])
-    pre = order[1].reshape(NY * LINE, 2 * NX * STATES)
+    def add(sums, axis, more):
+        sums[axis] = more if sums[axis] is None else sums[axis] + more
+
+    def other(axis, value):
+        order[axis] = value.reshape(8, LINE, 2 * NX * STATES)
+        reorder(order.at[axis], order.at[1 - axis])
+        return order[1 - axis].reshape(8 * LINE, 2 * NX * STATES)
+
+    pre = [None, None]
+    for q in ORDER:
+        w_steps[0][q](STEPS)
+        p = W_CHUNKS[0][q]
+        add(pre, AXIS[q], nt(units(0, p), states(feats, p)))
+    pre = other(0, pre[0]) + pre[1]
     tanh = jnp.tanh(GELU_A * (pre + GELU_B * pre * pre * pre))
     hidden = 0.5 * pre * (1.0 + tanh)
     slope = 0.5 * (1.0 + tanh) + 0.5 * pre * (1.0 - tanh * tanh) * (GELU_A * (1.0 + 3.0 * GELU_B * pre * pre))
-    hold[0] = hidden
-    hold[1] = slope
-    hidden_t[...] = hidden.T.astype(BF16).reshape(2, NX * STATES, NY * LINE)
-
-    mark("i_partial")
-    for q, p in enumerate(O_CHUNKS):
-        cross[:, :, p] = nn(hidden_t[1 - c], units(1, p)).astype(BF16).reshape(NX, STATES, p.stop - p.start)
-        send(cross.at[:, :, p], crossed.at[:, :, p], sent.at[6], r_cross.at[q], partner)
-    mark("j_rs")
-    for q, p in enumerate(O_CHUNKS):
-        partial[:, :, p] = nn(hidden_t[c], units(1, p)).reshape(NX, STATES, p.stop - p.start)
+    hold[1] = hidden
+    hold[2] = slope
+    hold[0] = other(1, hidden)
+    for axis in range(2):
+        hidden_t[axis] = hold[axis].T.astype(BF16).reshape(2, NX * STATES, 8 * LINE)
+
+    def to_chips(q):
+        p = O_CHUNKS[q]
         wait_all(crossed.at[:, :, p], r_cross.at[q])
         for k in (2, 1, 3):
             px = around(x, k, NX)
             to_x[px, :, p] = (partial[px, :, p] + crossed[px, :, p].astype(F32)).astype(BF16)
             send(to_x.at[px, :, p], from_x.at[x, :, p], sent.at[7], r_sum.at[q], x_peer(k))
+
+    mark("i_partial")
+    before = None
+    for q in ORDER:
+        w_steps[1][q](STEPS)
+        p = O_CHUNKS[q]
+        cross[:, :, p] = nn(hidden_t[AXIS[q], 1 - c], units(1, p)).astype(BF16).reshape(NX, STATES, p.stop - p.start)
+        send(cross.at[:, :, p], crossed.at[:, :, p], sent.at[6], r_cross.at[q], partner)
+        partial[:, :, p] = nn(hidden_t[AXIS[q], c], units(1, p)).reshape(NX, STATES, p.stop - p.start)
+        if before is not None:
+            to_chips(before)
+        before = q
+    mark("j_rs")
+    to_chips(before)
     mark("k_loss")
     lost = jnp.zeros((1, 1), F32)
-    for q, p in enumerate(O_CHUNKS):
+    for q in ORDER:
+        p = O_CHUNKS[q]
         wait_all(from_x.at[0:3, :, p], r_sum.at[q])
         summed = partial[x, :, p] + crossed[x, :, p].astype(F32)
         for k in range(1, NX):
@@ -268,7 +294,7 @@
     stores = [pltpu.make_async_copy(predicted, predicted_h, s_in.at[5])]
     stores[0].start()
     def ring_sum(g, q, p):
-        pos, n, to = ring[g]
+        pos, n, to = ring[AXIS[q]]
         copies = {}
 
         def term(move):
@@ -300,63 +326,63 @@
         return step, last
 
     sums_of = {g: [ring_sum(g, q, p) for q, p in enumerate(W_CHUNKS[g])] for g in (1, 0)}
-    hidden_b = hold[0].astype(BF16)
-
-    def backward(q, total):
+    hidden_b = [hold[axis].astype(BF16) for axis in range(2)]
+    hidden_grad = [None, None]
+
+    def backward(q):
         p = O_CHUNKS[q]
-        wait_all(values_grad.at[1 - c, :, :, p], r_cross.at[4 + q])
+        wait_all(values_grad.at[1 - c, :, :, p], r_cross.at[6 + q])
         grad = states(values_grad, p)
-        mine[1, :, :, p] = nn(hidden_b, grad).reshape(NY, LINE, p.stop - p.start)
-        for step, last in sums_of[1][(0, 2, 2, 4)[q] : (2, 2, 4, 6)[q]]:
-            step(0)
-        more = nt(units(1, p), grad)
-        return more if total is None else total + more
+        mine[1, :, :, p] = nn(hidden_b[AXIS[q]], grad).reshape(8, LINE, p.stop - p.start)
+        sums_of[1][q][0](0)
+        add(hidden_grad, AXIS[q], nt(units(1, p), grad))
 
     mark("l_ag")
-    hidden_grad = None
-    for q, p in enumerate(O_CHUNKS):
+    before = None
+    for q in ORDER:
+        p = O_CHUNKS[q]
         wait_all(from_x.at[0:3, :, p], r_grad.at[q])
         block = values_grad.at[c, :, :, p]
-        send(block, block, sent.at[9], r_cross.at[4 + q], partner)
-        if q:
-            hidden_grad = backward(q - 1, hidden_grad)
+        send(block, block, sent.at[9], r_cross.at[6 + q], partner)
+        if before is not None:
+            backward(before)
+        before = q
     mark("m_gout")
-    hidden_grad = backward(3, hidden_grad)
+    backward(before)
     mark("n_hgrad")
-    order[1] = (hidden_grad * hold[1]).reshape(NY, LINE, 2 * NX * STATES)
-    reorder(order.at[1], order.at[0])
-    pre_grad = order[0].reshape(NZ * LINE, 2 * NX * STATES).astype(BF16)
+    pre_grad = (other(0, hidden_grad[0]) + hidden_grad[1]) * hold[2]
+    pre_grad = [other(1, pre_grad).astype(BF16), pre_grad.astype(BF16)]
     mark("p_gin")
-    for h, piece in enumerate(PIECES):
-        mine[0, :, :, piece] = nn(pre_grad, states(feats, piece)).reshape(NZ, LINE, piece.stop - piece.start)
-        for step, last in sums_of[0][2 * h : 2 * h + 2]:
-            step(0)
+    for q in ORDER:
+        p = W_CHUNKS[0][q]
+        mine[0, :, :, p] = nn(pre_grad[AXIS[q]], states(feats, p)).reshape(8, LINE, p.stop - p.start)
+        sums_of[0][q][0](0)
     mark("r_zring")
     for k in range(1, STEPS):
         for g in (1, 0):
-            for step, last in sums_of[g]:
-                step(k)
+            for q in ORDER:
+                sums_of[g][q][0](k)
     mark("s_xsend")
-    for h, (piece, place) in enumerate(zip(PIECES, PLACES)):
-        for g in (1, 0):
-            pos, n, peer = line[g]
-            for q in range(2 * h, 2 * h + 2):
-                p = W_CHUNKS[g][q]
-                pack[g, :, p] = sums_of[g][q][1]()
+    for g in (1, 0):
+        for q in ORDER:
+            pos, n, peer = line[AXIS[q]]
+            piece, place = PIECES[g][q], PLACES[g][q]
+            pack[g, :, W_CHUNKS[g][q]] = sums_of[g][q][1]()
             for j in range(8):
                 line_send[g, j, :, place] = fold(pack[g, ROWS * j : ROWS * (j + 1), piece])
             for k in FAR_FIRST:
                 send(
                     line_send.at[g, around(pos, k, n), :, place], line_recv.at[g, pos, :, place],
-                    sent.at[12 + g], r_line.at[g, h], peer(k),
+                    sent.at[12 + g], r_line.at[g, q], peer(k),
                 )
             line_recv[g, pos, :, place] = line_send[g, pos, :, place]
     mark("t_xrecv")
     squares = jnp.zeros((1, 1), F32)
-    for h, (piece, place) in enumerate(zip(PIECES, PLACES)):
-        for g in (1, 0):
-            to, width = ((grad_in, INW), (grad_out, OUTW))[g]
-            wait_all(line_recv.at[g, 0:7, :, place], r_line.at[g, h])
+    for g in (1, 0):
+        to, width = ((grad_in, INW), (grad_out, OUTW))[g]
+        for q in ORDER:
+            piece, place = PIECES[g][q], PLACES[g][q]
+            wait_all(line_recv.at[g, 0:7, :, place], r_line.at[g, q])
             own = line_recv[g, 0, :, place].astype(F32)
             for j in range(1, 8):
                 own = own + line_recv[g, j, :, place].astype(F32)
@@ -367,10 +393,9 @@
                 to[rows, at:stop] = value[:, : stop - at]
 
             unfold(own, put)
-            if h == len(PIECES) - 1:
-                stores.append(pltpu.make_async_copy(to, (grad_in_h, grad_out_h)[g], s_in.at[6 + g]))
-                stores[-1].start()
-                squares = squares + jnp.sum(to[...] * to[...], keepdims=True)
+        stores.append(pltpu.make_async_copy(to, (grad_in_h, grad_out_h)[g], s_in.at[6 + g]))
+        stores[-1].start()
+        squares = squares + jnp.sum(to[...] * to[...], keepdims=True)
 
     mark("u_ar")
     lane = lax.broadcasted_iota(jnp.int32, (1, 128), 1)
@@ -468,14 +493,14 @@
         pltpu.VMEM((2, 8, LINE, WIDE), BF16),
         pltpu.VMEM((2, NX, STATES, WIDE), BF16),
         pltpu.VMEM((2, NX, STATES, WIDE), BF16),
-        pltpu.VMEM((2, NX * STATES, 8 * LINE), BF16),
+        pltpu.VMEM((2, 2, NX * STATES, 8 * LINE), BF16),
         pltpu.VMEM((NX, STATES, WIDE_OUT), F32),
         pltpu.VMEM((NX, STATES, WIDE_OUT), BF16),
         pltpu.VMEM((NX, STATES, WIDE_OUT), BF16),
         pltpu.VMEM((NX, STATES, WIDE_OUT), BF16),
         pltpu.VMEM((NX, STATES, WIDE_OUT), BF16),
         pltpu.VMEM((STATES, WIDE_OUT), F32),
-        pltpu.VMEM((2, 8 * LINE, 2 * NX * STATES), F32),
+        pltpu.VMEM((3, 8 * LINE, 2 * NX * STATES), F32),
         pltpu.VMEM((2, 8, LINE, 2 * NX * STATES), F32),
         pltpu.VMEM((2, 8, LINE, WIDE), F32),
         pltpu.VMEM((2, 7, LINE, WIDE), BF16),
@@ -488,7 +513,7 @@
         dma((9,)),
         dma((16,)),
     ]
-    for shape in ((2, 3), (2, 6, 8), (2,), (8,), (4,), (4,), (2, 3), (2,)):
+    for shape in ((2, 6), (2, 6, 8), (2,), (12,), (6,), (6,), (2, 6), (2,)):
         scratch.append(dma(shape))
     made = (
         jax.ShapeDtypeStruct((STATES, OUTW), BF16),

time: 82.7 us -> 79.5 us (0.961)
  Pallas kernels: 81.9 us -> 78.7 us
    pallas_call x1, Pallas kernels: 80.2 us -> 77 us  [body(): pl.pallas_call(kernel, name='step', out_shape=made, in_specs=[hbm] * 5, o...]
where the time goes in v6:
time: 79.5 us; the launch traced here: 79.3 us
  Pallas kernels  78.7 us (99%)
    pallas_call x1, Pallas kernels, body(): pl.pallas_call(kernel, name='step', out_shape=made, in_specs=[hbm] * 5, o...  77 us
    pallas_call x1, Pallas kernels, body(): pl.pallas_call(finish, name='finish', out_shape=outs, in_specs=[hbm] * 4,...  1.74 us

profile of v6, /device:TPU:1, one launch (start us, length us, event | category | flops | bytes accessed | tf_op | source)
XLA Modules:
  0.0 79.3 jit_solution(14388334931172498952)
XLA Ops:
  0.6 77.0 %step.1 = (bf16[16,2652]{1,0:T(8,128)(2,1)}, f32[3,2704]{1,0:T(4,128)}, f32[3,2652]{1,0:T(4,128)}, f32[1,128]{1,0:T(1,128)}) custom-call(bf16[16,2652]{1,0:T(8,128)(2,1)} %ranges_h.1, s32[5,16]{1,0:T(8,128)} %bitcast.2, bf16[16,2652]{1,0:T(8,128)(2,1)} %targets_h.1, bf16[3,2704]{1,0:T(4,128)(2,1)} %w_in_h.1, bf16[3,2652]{1,0:T(4,128)(2,1)} %w_out_h.1), custom_call_target="tpu_custom_call" | custom-call | tf_op jit(solution)/shard_map/step/pallas_call | solution.py:524
  77.6 1.7 %finish.1 = (bf16[16,2652]{1,0:T(8,128)(2,1)}, f32[3,2704]{1,0:T(4,128)}, f32[3,2652]{1,0:T(4,128)}, f32[1,1]{1,0:T(1,128)}) custom-call(bf16[16,2652]{1,0:T(8,128)(2,1)} %get-tuple-element.12.predicted_i, f32[3,2704]{1,0:T(4,128)} %get-tuple-element.13.grad_in_i, f32[3,2652]{1,0:T(4,128)} %get-tuple-element.14.grad_out_i, f32[1,128]{1,0:T(1,128)} %get-tuple-element.15.sums_i), custom_call_target="tpu_custom_call" | custom-call | tf_op jit(solution)/shard_map/finish/pallas_call | solution.py:541

commit v7 on v6

--- a/solution.py
+++ b/solution.py
@@ -20,11 +20,11 @@
     return tuple(slice(128 * a, 128 * b) for a, b in zip(cuts, cuts[1:]))
 
 
-PIECES = (columns(0, 4, 8, 12, 16, 20, 22), columns(0, 4, 8, 10, 14, 18, 22))
-W_CHUNKS = (PIECES[0], columns(0, 4, 8, 10, 14, 18, 21))
+PIECES = (columns(0, 6, 12, 18, 22), columns(0, 6, 10, 16, 22))
+W_CHUNKS = (PIECES[0], columns(0, 6, 10, 16, 21))
 O_CHUNKS = W_CHUNKS[1]
-AXIS = (0, 0, 0, 1, 1, 1)
-ORDER = (0, 3, 1, 4, 2, 5)
+AXIS = (0, 0, 1, 1)
+ORDER = (0, 2, 1, 3)
 PLACES = tuple(tuple(slice(p.start * 3 // 2, p.stop * 3 // 2) for p in pieces) for pieces in PIECES)
 PACKED = WIDE * 3 // 2
 
@@ -120,12 +120,31 @@
         pl.semaphore_signal(barrier, inc=1, device_id=device, device_id_type=MESH)
 
     mark("b_stage")
-    whole = OUTW // 128 * 128
-    for i, (w, width) in enumerate(((w_in, INW), (w_out, OUTW))):
+    def put_on_stage(i):
+        w, width = ((w_in, INW), (w_out, OUTW))[i]
         loads[i].wait()
         rows = jnp.concatenate([w[...].astype(F32), jnp.zeros((ROWS, WIDE - width), F32)], axis=1)
         for p, place in zip(PIECES[i], PLACES[i]):
             stage[i, :, place] = fold(rows[:, p])
+
+    put_on_stage(0)
+    mark("c_barwait")
+    pl.semaphore_wait(barrier, len(near))
+
+    mark("d_xsend")
+    line = ((y, NY, y_peer), (z, NZ, z_peer))
+    ring = tuple(
+        (pos, n, (peer(sign), peer(-sign), peer(2 * sign))) for pos, n, peer in ((z, NZ, z_peer), (y, NY, y_peer))
+    )
+    for i in range(2):
+        if i == 1:
+            put_on_stage(1)
+        for q in ORDER:
+            pos, n, peer = line[AXIS[q]]
+            place = PLACES[i][q]
+            for k in FAR_FIRST:
+                send(stage.at[i, :, place], rows8.at[i, pos, :, place], sent.at[i], r_w.at[i, q], peer(k))
+    whole = OUTW // 128 * 128
     loads[2].wait()
     loads[3].wait()
     feats[c, x, :, :whole] = ranges[:, :whole]
@@ -139,21 +158,6 @@
     shown = nt(diagonal.astype(F32).astype(BF16), shown.astype(BF16))
     tail = jnp.concatenate([ranges[:, whole:].astype(F32), jnp.zeros((STATES, WIDE - OUTW), F32)], axis=1)
     feats[c, x, :, whole:] = (tail + shown).astype(BF16)
-
-    mark("c_barwait")
-    pl.semaphore_wait(barrier, len(near))
-
-    mark("d_xsend")
-    line = ((y, NY, y_peer), (z, NZ, z_peer))
-    ring = tuple(
-        (pos, n, (peer(sign), peer(-sign), peer(2 * sign))) for pos, n, peer in ((z, NZ, z_peer), (y, NY, y_peer))
-    )
-    for i in range(2):
-        for q in ORDER:
-            pos, n, peer = line[AXIS[q]]
-            place = PLACES[i][q]
-            for k in FAR_FIRST:
-                send(stage.at[i, :, place], rows8.at[i, pos, :, place], sent.at[i], r_w.at[i, q], peer(k))
     for k in range(1, NX):
         send(feats.at[c, x], feats.at[c, x], sent.at[2], r_f.at[0], x_peer(k))
     for i in range(2):
@@ -331,7 +335,7 @@
 
     def backward(q):
         p = O_CHUNKS[q]
-        wait_all(values_grad.at[1 - c, :, :, p], r_cross.at[6 + q])
+        wait_all(values_grad.at[1 - c, :, :, p], r_cross.at[4 + q])
         grad = states(values_grad, p)
         mine[1, :, :, p] = nn(hidden_b[AXIS[q]], grad).reshape(8, LINE, p.stop - p.start)
         sums_of[1][q][0](0)
@@ -343,7 +347,7 @@
         p = O_CHUNKS[q]
         wait_all(from_x.at[0:3, :, p], r_grad.at[q])
         block = values_grad.at[c, :, :, p]
-        send(block, block, sent.at[9], r_cross.at[6 + q], partner)
+        send(block, block, sent.at[9], r_cross.at[4 + q], partner)
         if before is not None:
             backward(before)
         before = q
@@ -513,7 +517,7 @@
         dma((9,)),
         dma((16,)),
     ]
-    for shape in ((2, 6), (2, 6, 8), (2,), (12,), (6,), (6,), (2, 6), (2,)):
+    for shape in ((2, 4), (2, 4, 8), (2,), (8,), (4,), (4,), (2, 4), (2,)):
         scratch.append(dma(shape))
     made = (
         jax.ShapeDtypeStruct((STATES, OUTW), BF16),

time: 79.5 us -> 79.1 us (level)
  no operation moved by 1% of the time
where the time goes in v7:
time: 79.1 us; the launch traced here: 78.9 us
  Pallas kernels  78.3 us (99%)
    pallas_call x1, Pallas kernels, body(): pl.pallas_call(kernel, name='step', out_shape=made, in_specs=[hbm] * 5, o...  76.5 us
    pallas_call x1, Pallas kernels, body(): pl.pallas_call(finish, name='finish', out_shape=outs, in_specs=[hbm] * 4,...  1.74 us

profile of v7, /device:TPU:1, one launch (start us, length us, event | category | flops | bytes accessed | tf_op | source)
XLA Modules:
  0.0 78.9 jit_solution(10592243413325930120)
XLA Ops:
  0.6 76.5 %step.1 = (bf16[16,2652]{1,0:T(8,128)(2,1)}, f32[3,2704]{1,0:T(4,128)}, f32[3,2652]{1,0:T(4,128)}, f32[1,128]{1,0:T(1,128)}) custom-call(bf16[16,2652]{1,0:T(8,128)(2,1)} %ranges_h.1, s32[5,16]{1,0:T(8,128)} %bitcast.2, bf16[16,2652]{1,0:T(8,128)(2,1)} %targets_h.1, bf16[3,2704]{1,0:T(4,128)(2,1)} %w_in_h.1, bf16[3,2652]{1,0:T(4,128)(2,1)} %w_out_h.1), custom_call_target="tpu_custom_call" | custom-call | tf_op jit(solution)/shard_map/step/pallas_call | solution.py:528
  77.2 1.7 %finish.1 = (bf16[16,2652]{1,0:T(8,128)(2,1)}, f32[3,2704]{1,0:T(4,128)}, f32[3,2652]{1,0:T(4,128)}, f32[1,1]{1,0:T(1,128)}) custom-call(bf16[16,2652]{1,0:T(8,128)(2,1)} %get-tuple-element.12.predicted_i, f32[3,2704]{1,0:T(4,128)} %get-tuple-element.13.grad_in_i, f32[3,2652]{1,0:T(4,128)} %get-tuple-element.14.grad_out_i, f32[1,128]{1,0:T(1,128)} %get-tuple-element.15.sums_i), custom_call_target="tpu_custom_call" | custom-call | tf_op jit(solution)/shard_map/finish/pallas_call | solution.py:545

commit v8 on v7

--- a/solution.py
+++ b/solution.py
@@ -25,6 +25,7 @@
 O_CHUNKS = W_CHUNKS[1]
 AXIS = (0, 0, 1, 1)
 ORDER = (0, 2, 1, 3)
+VALUES_ORDER = (2, 0, 3, 1)
 PLACES = tuple(tuple(slice(p.start * 3 // 2, p.stop * 3 // 2) for p in pieces) for pieces in PIECES)
 PACKED = WIDE * 3 // 2
 
@@ -252,8 +253,9 @@
     slope = 0.5 * (1.0 + tanh) + 0.5 * pre * (1.0 - tanh * tanh) * (GELU_A * (1.0 + 3.0 * GELU_B * pre * pre))
     hold[1] = hidden
     hold[2] = slope
-    hold[0] = other(1, hidden)
-    for axis in range(2):
+    for axis in (1, 0):
+        if axis == 0:
+            hold[0] = other(1, hidden)
         hidden_t[axis] = hold[axis].T.astype(BF16).reshape(2, NX * STATES, 8 * LINE)
 
     def to_chips(q):
@@ -266,7 +268,7 @@
 
     mark("i_partial")
     before = None
-    for q in ORDER:
+    for q in VALUES_ORDER:
         w_steps[1][q](STEPS)
         p = O_CHUNKS[q]
         cross[:, :, p] = nn(hidden_t[AXIS[q], 1 - c], units(1, p)).astype(BF16).reshape(NX, STATES, p.stop - p.start)
@@ -279,7 +281,7 @@
     to_chips(before)
     mark("k_loss")
     lost = jnp.zeros((1, 1), F32)
-    for q in ORDER:
+    for q in VALUES_ORDER:
         p = O_CHUNKS[q]
         wait_all(from_x.at[0:3, :, p], r_sum.at[q])
         summed = partial[x, :, p] + crossed[x, :, p].astype(F32)
@@ -343,7 +345,7 @@
 
     mark("l_ag")
     before = None
-    for q in ORDER:
+    for q in VALUES_ORDER:
         p = O_CHUNKS[q]
         wait_all(from_x.at[0:3, :, p], r_grad.at[q])
         block = values_grad.at[c, :, :, p]

time: 79.1 us -> 80.2 us (1.014)
  Pallas kernels: 78.3 us -> 79.3 us
    pallas_call x1, Pallas kernels: 76.5 us -> 77.6 us  [body(): pl.pallas_call(kernel, name='step', out_shape=made, in_specs=[hbm] * 5, o...]
where the time goes in v8:
time: 80.2 us; the launch traced here: 80 us
  Pallas kernels  79.3 us (99%)
    pallas_call x1, Pallas kernels, body(): pl.pallas_call(kernel, name='step', out_shape=made, in_specs=[hbm] * 5, o...  77.6 us
    pallas_call x1, Pallas kernels, body(): pl.pallas_call(finish, name='finish', out_shape=outs, in_specs=[hbm] * 4,...  1.74 us

profile of v8, /device:TPU:1, one launch (start us, length us, event | category | flops | bytes accessed | tf_op | source)
XLA Modules:
  0.0 80.0 jit_solution(10901503339271013026)
XLA Ops:
  0.6 77.6 %step.1 = (bf16[16,2652]{1,0:T(8,128)(2,1)}, f32[3,2704]{1,0:T(4,128)}, f32[3,2652]{1,0:T(4,128)}, f32[1,128]{1,0:T(1,128)}) custom-call(bf16[16,2652]{1,0:T(8,128)(2,1)} %ranges_h.1, s32[5,16]{1,0:T(8,128)} %bitcast.2, bf16[16,2652]{1,0:T(8,128)(2,1)} %targets_h.1, bf16[3,2704]{1,0:T(4,128)(2,1)} %w_in_h.1, bf16[3,2652]{1,0:T(4,128)(2,1)} %w_out_h.1), custom_call_target="tpu_custom_call" | custom-call | tf_op jit(solution)/shard_map/step/pallas_call | solution.py:530
  78.2 1.7 %finish.1 = (bf16[16,2652]{1,0:T(8,128)(2,1)}, f32[3,2704]{1,0:T(4,128)}, f32[3,2652]{1,0:T(4,128)}, f32[1,1]{1,0:T(1,128)}) custom-call(bf16[16,2652]{1,0:T(8,128)(2,1)} %get-tuple-element.12.predicted_i, f32[3,2704]{1,0:T(4,128)} %get-tuple-element.13.grad_in_i, f32[3,2652]{1,0:T(4,128)} %get-tuple-element.14.grad_out_i, f32[1,128]{1,0:T(1,128)} %get-tuple-element.15.sums_i), custom_call_target="tpu_custom_call" | custom-call | tf_op jit(solution)/shard_map/finish/pallas_call | solution.py:547
